TPU v7x, 256 devices: a whole 4x4x8 slice. The times are simulated.
256 devices in a mesh: band: 8 (over z_lo, x), vis: 32 (over y, z_hi, core).
Axes of the slice: x: 4, y: 4, z: 8 (z_hi: 4, z_lo: 2; z = z_hi * 2 + z_lo), core: 2. Of those that a mesh axis runs over, the one named last changes fastest.
Arguments:
- sky_image: float32 [4096, 4096], P(('band', 'vis')), as said below
- coef_dual: float32 [4, 2048, 2048], P(None, ('band', 'vis')), may hold values from -12 to 12
- vis_dual: float32 [8, 32, 32, 4, 2, 32], P('band', 'vis'), may hold values from -12 to 12
- visibilities: float32 [8, 32, 32, 4, 2, 32], P('band', 'vis')
- kernel_blocks: bfloat16 [8, 32, 32, 4, 2, 32, 128], P('band', 'vis'), may hold values from -0.5 to 0.5
- tile_rows: int32 [8, 32, 32, 4], P('band', 'vis'), may hold values from 0 to 511
- tile_counts: int32 [8, 32, 32], P('band', 'vis'), may hold values from 1 to 4, as said below
Outputs:
- new_image: float32 [4096, 4096], P(('band', 'vis'))
- new_coef_dual: float32 [4, 2048, 2048], P(None, ('band', 'vis'))
- new_vis_dual: float32 [8, 32, 32, 4, 2, 32], P('band', 'vis')
Inputs may be any that keep to these rules, and one draw needn't show every extreme that they name: `sky_image`: nonnegative. `tile_counts`: in every band some owner q has all 4 slots live from every device of that band.
All inputs are finite; a program needn't handle non-finite values.
Results may differ from a plain program's by a relative error of at most 0.0018.
Values may be sent and summed in bfloat16 or wider, within the bound.
A program may use at most 64 MiB of HBM per device.

v0:
```python
import functools
import math

import jax
import jax.numpy as jnp
import numpy as np
from jax import lax
from jax.experimental import pallas as pl
from jax.experimental.pallas import tpu as pltpu
from jax.sharding import PartitionSpec as P

IMG = 4096
NB = 8
NV = 32
MESH_ID = pl.DeviceIdType.MESH
highest = lax.Precision.HIGHEST
f32 = jnp.float32
bf16 = jnp.bfloat16

low_taps = (
    -0.010597401784997278,
    0.032883011666982945,
    0.030841381835986965,
    -0.18703481171888114,
    -0.02798376941698385,
    0.6308807679295904,
    0.7148465705525415,
    0.23037781330885523,
)
high_taps = tuple(((-1.0) ** offset * low_taps[7 - offset] for offset in range(8)))


def halves_of(table):
    high = table.astype(bf16)
    low = (table - high.astype(np.float64)).astype(bf16)
    return high, low


def dft512_tables():
    index = np.arange(512)
    angle = 2.0 * np.pi / 512 * (index[:, None] * index[None, :] % 512)
    return halves_of(np.concatenate([np.cos(angle), np.sin(angle)], axis=0))


def dft128_table():
    index = np.arange(128)
    angle = 2.0 * np.pi / 128 * (index[:, None] * index[None, :] % 128)
    return (np.concatenate([np.cos(angle), np.sin(angle)], axis=1) / IMG).astype(np.float32)


def row_twist():
    angle = 2.0 * np.pi / IMG * (np.arange(32)[:, None] * np.arange(128)[None, :] % IMG)
    return np.stack([np.cos(angle), np.sin(angle)], axis=1).astype(np.float32)


def wavelet_tables():
    up = np.zeros((512, 256))
    down = np.zeros((384, 256))
    rows_up = np.zeros((2, 16, 32))
    rows_down = np.zeros((16, 24))
    for tap in range(8):
        for side, taps in ((0, low_taps), (1, high_taps)):
            for k in range(128):
                down[2 * k + tap, 128 * side + k] = taps[tap]
            for k in range(-128, 128):
                if 0 <= 2 * k + tap < 256:
                    up[256 * side + 128 + k, 2 * k + tap] = taps[tap]
            for k in range(8):
                rows_down[8 * side + k, 2 * k + tap] = taps[tap]
            for k in range(-3, 8):
                if 0 <= 2 * k + tap < 16:
                    for part in range(2):
                        spot = 8 * side + k if k >= 0 else 16 + 3 * (part + 2 * side) + k + 3
                        rows_up[part, 2 * k + tap, spot] = taps[tap]
    sides = np.zeros((48, 32))
    sides[0:32] = rows_up.reshape(32, 32)
    sides[32:48, 0:24] = rows_down
    return tuple(part for table in (up, down, sides) for part in halves_of(table))


def lane_order():
    place = np.zeros((128, 128), np.float32)
    for t in range(128):
        place[(t % 8) * 16 + t // 8, t] = 1.0
    return place.astype(bf16)


def times(pair, cosine, sine):
    re, im = pair
    if abs(sine) < 1e-12:
        if cosine > 0:
            return pair
        return (-re, None if im is None else -im)
    if abs(cosine) < 1e-12:
        if im is None:
            return (None, re if sine > 0 else -re)
        return (-im, re) if sine > 0 else (im, -re)
    cosine, sine = np.float32(cosine), np.float32(sine)
    if im is None:
        return (re * cosine, re * sine)
    return (re * cosine - im * sine, re * sine + im * cosine)


def plus(a, b):
    if a is None:
        return b
    return a if b is None else a + b


def minus(a, b):
    if b is None:
        return a
    return -b if a is None else a - b


def small_dft(values, sign):
    count = len(values)
    if count == 1:
        return values
    even = small_dft(values[0::2], sign)
    odd = small_dft(values[1::2], sign)
    out = [None] * count
    for k in range(count // 2):
        angle = sign * 2.0 * math.pi * k / count
        turned = times(odd[k], math.cos(angle), math.sin(angle))
        out[k] = (plus(even[k][0], turned[0]), plus(even[k][1], turned[1]))
        out[k + count // 2] = (minus(even[k][0], turned[0]), minus(even[k][1], turned[1]))
    return out


def swap_groups(arrays):
    arrays = list(arrays)
    lane = lax.broadcasted_iota(jnp.int32, arrays[0].shape, arrays[0].ndim - 1)
    axis = arrays[0].ndim - 1
    for bit in range(3):
        shift = 16 << bit
        upper = (lane // shift) % 2 == 1
        for j in range(8):
            other = j | (1 << bit)
            if other == j:
                continue
            low, high = arrays[j], arrays[other]
            arrays[j] = jnp.where(upper, pltpu.roll(high, shift, axis), low)
            arrays[other] = jnp.where(upper, high, pltpu.roll(low, 128 - shift, axis))
    return arrays


def dot(a, b):
    return jnp.dot(a, b, preferred_element_type=f32)


def dot_nt(a, b):
    return lax.dot_general(a, b, (((1,), (1,)), ((), ())), preferred_element_type=f32)


def halves(value):
    high = value.astype(bf16)
    return high, (value - high.astype(f32)).astype(bf16)


def by_table(value, high, low):
    value_high, value_low = halves(value)
    return dot(value_high, high) + dot(value_low, high) + dot(value_high, low)


def table_by(high, low, value):
    value_high, value_low = halves(value)
    return dot(high, value_high) + dot(high, value_low) + dot(low, value_high)


def greet(vis_me, band_me, neighbours):
    barrier = pltpu.get_barrier_semaphore()

    def vis_signal(d, carry):
        pl.semaphore_signal(
            barrier, inc=1, device_id={"vis": vis_me ^ d}, device_id_type=MESH_ID
        )
        return carry

    def band_signal(d, carry):
        pl.semaphore_signal(
            barrier, inc=1, device_id={"band": band_me ^ d}, device_id_type=MESH_ID
        )
        return carry

    for neighbour in neighbours:
        pl.semaphore_signal(barrier, inc=1, device_id=neighbour, device_id_type=MESH_ID)
    lax.fori_loop(1, NV, vis_signal, 0)
    lax.fori_loop(1, NB, band_signal, 0)
    return barrier


def launch(sent, landed, sems, axis, count, me, same=False):
    def body(d, carry):
        peer = me ^ d
        pltpu.make_async_remote_copy(
            src_ref=sent if same else sent.at[peer],
            dst_ref=landed.at[me],
            send_sem=sems.at[0],
            recv_sem=sems.at[1],
            device_id={axis: peer},
            device_id_type=MESH_ID,
        ).start()
        return carry

    lax.fori_loop(1, count, body, 0)
    landed[me] = sent[...] if same else sent[me]


def to_neighbour(sent, landed, sems, neighbour):
    copy = pltpu.make_async_remote_copy(
        src_ref=sent,
        dst_ref=landed,
        send_sem=sems.at[0],
        recv_sem=sems.at[1],
        device_id=neighbour,
        device_id_type=MESH_ID,
    )
    copy.start()
    return copy


def arrived(landed, sems, count):
    part = landed.at[pl.ds(0, count - 1)]
    pltpu.make_async_copy(part, part, sems.at[1]).wait()


def drained(landed, sems, count):
    part = landed.at[pl.ds(0, count - 1)]
    pltpu.make_async_copy(part, part, sems.at[0]).wait()


def step_kernel(*refs):
    names = INPUTS + OUTPUTS + list(SCRATCH)
    r = dict(zip(names, refs))
    vis_me, band_me = lax.axis_index("vis"), lax.axis_index("band")
    me = band_me * NV + vis_me
    following = (me + 1) % (NB * NV)
    preceding = (me + NB * NV - 1) % (NB * NV)
    following = {"band": following // NV, "vis": following % NV}
    preceding = {"band": preceding // NV, "vis": preceding % NV}
    copies = {}
    for place, name in enumerate(STAGED):
        copies[name] = pltpu.make_async_copy(r[name], r["here_" + name], r["sem_in"].at[place])
        copies[name].start()

    def staged(name):
        if name in copies:
            copies.pop(name).wait()
        return r["here_" + name]

    barrier = greet(vis_me, band_me, (following, preceding))

    weights, places, sent_a, got_a = r["weights"], r["places"], r["sent_a"], r["got_a"]
    kernels = staged("kernels")
    for q in range(NV):
        part = dot(weights[q], kernels[q])
        sent_a[q] = jnp.concatenate([part, places[q]], axis=0).astype(bf16)
    pl.semaphore_wait(barrier, NV + NB)
    launch(sent_a, got_a, r["sem_a"], "vis", NV, vis_me)
    coef_copy = to_neighbour(r["coef_rows"], r["got_coef"], r["sem_coef"], following)

    coef, sky = staged("coef"), staged("sky")
    sides_hi, sides_lo = r["sides_hi"], r["sides_lo"]
    up_hi, up_lo = staged("up_hi"), staged("up_lo")
    coef_copy.wait_recv()
    rows_up = []
    for part in range(2):
        rows = slice(16 * part, 16 * part + 16)
        stack = jnp.concatenate([coef[part], coef[part + 2], r["got_coef"][...]], axis=0)
        rows_up.append(table_by(sides_hi[rows, :], sides_lo[rows, :], stack))
    stack = []
    for n in range(16):
        parts = []
        for field in rows_up:
            for block in ((n + 15) % 16, n):
                parts.append(field[:, 128 * block : 128 * block + 128])
        stack.append(jnp.concatenate(parts, axis=1))
    smooth = by_table(jnp.concatenate(stack, axis=0), up_hi[...], up_lo[...])
    raw = r["raw_here"]
    for n in range(16):
        cols = slice(256 * n, 256 * n + 256)
        raw[:, cols] = sky[:, cols] - smooth[16 * n : 16 * n + 16]
    arrived(got_a, r["sem_a"], NV)

    order, onehot, sent_b, got_b = r["order"], r["onehot"], r["sent_b"], r["got_b"]
    contrib = got_a[:, 0:8, :].astype(f32).reshape(256, 128).astype(bf16)
    where_to = got_a[:, 8:16, :].astype(f32).reshape(256, 128)
    lane = lax.broadcasted_iota(jnp.int32, (256, 128), 1).astype(f32)
    is_imag = lax.broadcasted_iota(jnp.int32, (256, 128), 0) % 2 == 1
    hots = [(where_to == lane + float(128 * g - 256)).astype(f32) for g in range(4)]
    for g in range(4):
        onehot[:, 128 * g : 128 * g + 128] = hots[g].astype(bf16)
    real_hots = [jnp.where(is_imag, 0.0, h).astype(bf16) for h in hots]
    imag_hots = [jnp.where(is_imag, h, 0.0).astype(bf16) for h in hots]
    turned = dot_nt(order[...], contrib).astype(bf16)
    for c, some in ((0, real_hots), (1, imag_hots)):
        for g in range(4):
            grid = dot(turned, some[g]).astype(bf16)
            for low in range(8):
                sent_b[low * 4 + g, c] = grid[16 * low : 16 * low + 16]
    launch(sent_b, got_b, r["sem_b"], "vis", NV, vis_me)
    table_hi, table_lo = staged("table_hi"), staged("table_lo")
    arrived(got_b, r["sem_b"], NV)

    sent_c, got_c = r["sent_c"], r["got_c"]
    spread = jnp.concatenate(
        [got_b[:, 0].reshape(512, 128), got_b[:, 1].reshape(512, 128)], axis=1
    )
    both = dot(table_hi[...], spread) + dot(table_lo[...], spread)
    sent_c[:, 0] = (both[:512, :128] - both[512:, 128:]).astype(bf16).reshape(NV, 16, 128)
    sent_c[:, 1] = (both[512:, :128] + both[:512, 128:]).astype(bf16).reshape(NV, 16, 128)
    launch(sent_c, got_c, r["sem_c"], "vis", NV, vis_me)
    arrived(got_c, r["sem_c"], NV)

    sent_d, got_d, twist_col = r["sent_d"], r["got_d"], r["twist_col"]
    for g in range(4):
        values = []
        for low in range(8):
            re = got_c[low * 4 + g, 0].astype(f32)
            im = got_c[low * 4 + g, 1].astype(f32)
            cosine, sine = twist_col[low, 0], twist_col[low, 1]
            values.append((re * cosine - im * sine, re * sine + im * cosine))
        values = small_dft(values, 1.0)
        for b in range(NB):
            for c in range(2):
                sent_d[b, c, :, 128 * g : 128 * g + 128] = values[b][c].astype(sent_d.dtype)
    launch(sent_d, got_d, r["sem_d"], "band", NB, band_me)
    arrived(got_d, r["sem_d"], NB)

    mid, table128, twist_row = r["mid"], r["table128"], r["twist_row"]
    for g in range(4):
        for c in range(2):
            parts = swap_groups(
                [got_d[b, c, :, 128 * g : 128 * g + 128].astype(f32) for b in range(NB)]
            )
            for a in range(8):
                mid[g * 8 + a, c] = parts[a]
    lanes = jnp.dot(
        mid[...].reshape(1024, 128), table128[...], precision=highest, preferred_element_type=f32
    ).reshape(32, 2, 16, 256)
    extrap = r["extrap"]
    for half in range(2):
        rows = slice(8 * half, 8 * half + 8)
        values = []
        for a in range(32):
            re = lanes[a, 0, rows, :128] - lanes[a, 1, rows, 128:]
            im = lanes[a, 0, rows, 128:] + lanes[a, 1, rows, :128]
            cosine, sine = twist_row[a, 0:1], twist_row[a, 1:2]
            values.append((re * cosine - im * sine, re * sine + im * cosine))
        values = small_dft(values, 1.0)
        for n in range(32):
            cols = slice(128 * n, 128 * n + 128)
            now = raw[rows, cols] - values[n][0]
            raw[rows, cols] = now
            extrap[rows, cols] = 2.0 * jnp.maximum(now, 0.0) - sky[rows, cols]
    image_copy = to_neighbour(extrap.at[pl.ds(0, 8)], r["got_rows"], r["sem_rows"], preceding)
    out_raw = pltpu.make_async_copy(raw, r["raw"], r["sem_out"].at[0])
    out_raw.start()

    sent_e, got_e = r["sent_e"], r["got_e"]
    for half in range(2):
        rows = slice(8 * half, 8 * half + 8)
        values = [(extrap[rows, 128 * n : 128 * n + 128], None) for n in range(32)]
        values = small_dft(values, -1.0)
        for a in range(32):
            re, im = values[a]
            cosine, sine = twist_row[a, 0:1], twist_row[a, 1:2]
            if im is None:
                mid[a, 0, rows] = re * cosine
                mid[a, 1, rows] = -re * sine
            else:
                mid[a, 0, rows] = re * cosine + im * sine
                mid[a, 1, rows] = im * cosine - re * sine
    lanes = jnp.dot(
        mid[...].reshape(1024, 128), table128[...], precision=highest, preferred_element_type=f32
    ).reshape(32, 2, 16, 256)
    for g in range(4):
        for c in range(2):
            parts = []
            for a in range(8):
                re, im = lanes[g * 8 + a, 0], lanes[g * 8 + a, 1]
                if c == 0:
                    parts.append(re[:, :128] + im[:, 128:])
                else:
                    parts.append(im[:, :128] - re[:, 128:])
            parts = swap_groups(parts)
            for b in range(NB):
                sent_e[b, c, :, 128 * g : 128 * g + 128] = parts[b].astype(sent_e.dtype)
    launch(sent_e, got_e, r["sem_e"], "band", NB, band_me)

    down_hi, down_lo = staged("down_hi"), staged("down_lo")
    image_copy.wait_recv()
    fields = jnp.concatenate([extrap[...], r["got_rows"][...]], axis=0)
    fields = table_by(sides_hi[32:48, 0:24], sides_lo[32:48, 0:24], fields)
    stack = []
    for n in range(16):
        if n < 15:
            stack.append(fields[:, 256 * n : 256 * n + 384])
        else:
            stack.append(jnp.concatenate([fields[:, 3840:4096], fields[:, 0:128]], axis=1))
    found = by_table(jnp.concatenate(stack, axis=0), down_hi[...], down_lo[...])
    coeffs = r["coeffs_here"]
    for n in range(16):
        cols = slice(128 * n, 128 * n + 128)
        block = found[16 * n : 16 * n + 16]
        coeffs[0, :, cols] = block[0:8, :128]
        coeffs[1, :, cols] = block[0:8, 128:]
        coeffs[2, :, cols] = block[8:16, :128]
        coeffs[3, :, cols] = block[8:16, 128:]
    abs_total = jnp.sum(jnp.abs(found))
    out_coeffs = pltpu.make_async_copy(coeffs, r["coeffs"], r["sem_out"].at[1])
    out_coeffs.start()
    arrived(got_e, r["sem_e"], NB)

    sent_f, got_f = r["sent_f"], r["got_f"]
    for g in range(4):
        values = []
        for b in range(NB):
            values.append(
                tuple(
                    got_e[b, c, :, 128 * g : 128 * g + 128].astype(f32) for c in range(2)
                )
            )
        values = small_dft(values, -1.0)
        for low in range(8):
            re, im = values[low]
            cosine, sine = twist_col[low, 0], twist_col[low, 1]
            sent_f[low * 4 + g, 0] = (re * cosine + im * sine).astype(sent_f.dtype)
            sent_f[low * 4 + g, 1] = (im * cosine - re * sine).astype(sent_f.dtype)
    launch(sent_f, got_f, r["sem_f"], "vis", NV, vis_me)
    arrived(got_f, r["sem_f"], NV)

    sent_g, got_g = r["sent_g"], r["got_g"]
    spread = jnp.concatenate(
        [got_f[:, 0].reshape(512, 128), got_f[:, 1].reshape(512, 128)], axis=1
    )
    if spread.dtype == f32:
        both = table_by(table_hi[...], table_lo[...], spread)
    else:
        both = dot(table_hi[...], spread) + dot(table_lo[...], spread)
    sent_g[:, 0] = (both[:512, :128] + both[512:, 128:]).astype(bf16).reshape(NV, 16, 128)
    sent_g[:, 1] = (both[:512, 128:] - both[512:, :128]).astype(bf16).reshape(NV, 16, 128)
    launch(sent_g, got_g, r["sem_g"], "vis", NV, vis_me)
    arrived(got_g, r["sem_g"], NV)

    sent_h, got_h = r["sent_h"], r["got_h"]
    picked = []
    for c in range(2):
        total = 0.0
        for g in range(4):
            piece = jnp.concatenate([got_g[low * 4 + g, c] for low in range(8)], axis=0)
            total = total + dot_nt(onehot[:, 128 * g : 128 * g + 128], piece)
        picked.append(total)
    tiles = jnp.where(is_imag, picked[1], picked[0]).astype(bf16)
    tiles = dot(tiles, order[...])
    sent_h[...] = tiles.reshape(NV, 8, 128).astype(bf16)
    launch(sent_h, got_h, r["sem_h"], "vis", NV, vis_me)
    data_square = jnp.sum(r["live"][...] * r["vis_data"][...] * r["vis_data"][...])
    arrived(got_h, r["sem_h"], NV)

    row = lax.broadcasted_iota(jnp.int32, (8, 256), 0)
    slot = lax.broadcasted_iota(jnp.int32, (8, 256), 1) // 64
    on_real = row == 2 * slot
    on_imag = row == 2 * slot + 1
    from_real, from_imag = [], []
    for q in range(NV):
        product = dot_nt(got_h[q], kernels[q])
        from_real.append(jnp.sum(jnp.where(on_real, product, 0.0), axis=0, keepdims=True))
        from_imag.append(jnp.sum(jnp.where(on_imag, product, 0.0), axis=0, keepdims=True))
    from_real = jnp.concatenate(from_real, axis=0)
    from_imag = jnp.concatenate(from_imag, axis=0)
    imag_lane = (lax.broadcasted_iota(jnp.int32, (NV, 256), 1) // 32) % 2 == 1
    predicted = from_real + jnp.where(
        imag_lane, pltpu.roll(from_imag, 32, 1), -pltpu.roll(from_imag, 256 - 32, 1)
    )
    residual = r["live"][...] * (r["vis_state"][...] + predicted - r["vis_data"][...])
    resid_square = jnp.sum(residual * residual)

    sent_t, got_t, sent_u, got_u = r["sent_t"], r["got_t"], r["sent_u"], r["got_u"]
    spot = lax.broadcasted_iota(jnp.int32, (8, 128), 0)
    sent_t[...] = jnp.where(
        spot == 0, abs_total, jnp.where(spot == 1, resid_square, data_square)
    )
    launch(sent_t, got_t, r["sem_t"], "vis", NV, vis_me, same=True)
    arrived(got_t, r["sem_t"], NV)
    sent_u[...] = jnp.sum(got_t[...], axis=0)
    launch(sent_u, got_u, r["sem_u"], "band", NB, band_me, same=True)
    arrived(got_u, r["sem_u"], NB)
    totals = jnp.sum(got_u[...], axis=0)
    r["totals"][...] = totals
    radius = 0.5 * jnp.sqrt(totals[2:3, :] + 1e-06)
    size = jnp.sqrt(totals[1:2, :] + 1e-06)
    factor = 1.0 - jnp.minimum(1.0, radius / size)
    r["vis_new"][:, 0:128] = residual[:, 0:128] * factor
    r["vis_new"][:, 128:256] = residual[:, 128:256] * factor

    for copy in (coef_copy, image_copy):
        copy.wait_send()
    out_raw.wait()
    out_coeffs.wait()
    for name, landed, count in (
        ("a", got_a, NV), ("b", got_b, NV), ("c", got_c, NV), ("d", got_d, NB),
        ("e", got_e, NB), ("f", got_f, NV), ("g", got_g, NV), ("h", got_h, NV),
        ("t", got_t, NV), ("u", got_u, NB),
    ):
        drained(landed, r["sem_" + name], count)


STAGED = ["kernels", "coef", "sky", "up_hi", "up_lo", "table_hi", "table_lo", "down_hi", "down_lo"]
INPUTS = STAGED + [
    "coef_rows", "weights", "places", "live", "vis_state", "vis_data",
    "table128", "twist_row", "twist_col", "order", "sides_hi", "sides_lo",
]
OUTPUTS = ["raw", "coeffs", "vis_new", "totals"]
VIS_TILE = (NV, 2, 16, 128)
BAND_TILE = (NB, 2, 16, 512)
SCRATCH = dict(
    here_kernels=((NV, 256, 128), bf16),
    here_coef=((4, 8, 2048), f32),
    here_sky=((16, IMG), f32),
    here_up_hi=((512, 256), bf16),
    here_up_lo=((512, 256), bf16),
    here_table_hi=((1024, 512), bf16),
    here_table_lo=((1024, 512), bf16),
    here_down_hi=((384, 256), bf16),
    here_down_lo=((384, 256), bf16),
    sent_a=((NV, 16, 128), bf16), got_a=((NV, 16, 128), bf16),
    sent_b=(VIS_TILE, bf16), got_b=(VIS_TILE, bf16),
    sent_c=(VIS_TILE, bf16), got_c=(VIS_TILE, bf16),
    sent_d=(BAND_TILE, bf16), got_d=(BAND_TILE, bf16),
    sent_e=(BAND_TILE, f32), got_e=(BAND_TILE, f32),
    sent_f=(VIS_TILE, f32), got_f=(VIS_TILE, f32),
    sent_g=(VIS_TILE, bf16), got_g=(VIS_TILE, bf16),
    sent_h=((NV, 8, 128), bf16), got_h=((NV, 8, 128), bf16),
    sent_t=((8, 128), f32), got_t=((NV, 8, 128), f32),
    sent_u=((8, 128), f32), got_u=((NB, 8, 128), f32),
    got_coef=((16, 2048), f32), got_rows=((8, IMG), f32),
    raw_here=((16, IMG), f32), extrap=((16, IMG), f32), coeffs_here=((4, 8, 2048), f32),
    onehot=((256, 512), bf16), mid=((32, 2, 16, 128), f32),
    **{"sem_" + n: 2 for n in list("abcdefghtu") + ["coef", "rows", "out"]},
    sem_in=len(STAGED),
)


def step(inputs):
    anywhere = pl.BlockSpec(memory_space=pl.ANY)
    vmem = pl.BlockSpec(memory_space=pltpu.VMEM)
    scratch = []
    for what in SCRATCH.values():
        if isinstance(what, int):
            scratch.append(pltpu.SemaphoreType.DMA((what,)))
        else:
            scratch.append(pltpu.VMEM(*what))
    return pl.pallas_call(
        step_kernel,
        out_shape=(
            jax.ShapeDtypeStruct((16, IMG), f32),
            jax.ShapeDtypeStruct((4, 8, 2048), f32),
            jax.ShapeDtypeStruct((NV, 256), f32),
            jax.ShapeDtypeStruct((8, 128), f32),
        ),
        in_specs=[anywhere if name in STAGED else vmem for name in INPUTS],
        out_specs=(anywhere, anywhere, vmem, vmem),
        scratch_shapes=scratch,
        compiler_params=pltpu.CompilerParams(
            collective_id=0, has_side_effects=True, vmem_limit_bytes=56 * 2**20
        ),
    )(*[inputs[name] for name in INPUTS])


def local(sky_image, coef_dual, vis_dual, visibilities, kernel_blocks, tile_rows, tile_counts):
    kernels = kernel_blocks.reshape(NV, 256, 128)
    rows_here = tile_rows.reshape(NV, 4)
    counts = tile_counts.reshape(NV, 1)
    live = (jnp.arange(256, dtype=jnp.int32)[None, :] // 64 < counts).astype(f32)
    vis_data = visibilities.reshape(NV, 256)
    vis_state = vis_dual.reshape(NV, 256)

    wb = live * vis_state
    lane = jnp.arange(256, dtype=jnp.int32)
    imag_lane = (lane // 32) % 2 == 1
    crossed = jnp.where(imag_lane, -jnp.roll(wb, 32, axis=1), jnp.roll(wb, -32, axis=1))
    slot_row = jnp.arange(8, dtype=jnp.int32)
    same = (slot_row[:, None] // 2 == lane[None, :] // 64)[None]
    chosen = jnp.where((slot_row % 2 == 1)[None, :, None], crossed[:, None, :], wb[:, None, :])
    weights = jnp.where(same, chosen, 0.0).astype(bf16)

    place = (rows_here % 32) * 16 + rows_here // 32 - 256
    places = jnp.broadcast_to(
        jnp.repeat(place.astype(f32), 2, axis=1)[:, :, None], (NV, 8, 128)
    )

    low = jnp.arange(8, dtype=jnp.int32)[:, None]
    mu = lax.axis_index("vis") * 16 + jnp.arange(16, dtype=jnp.int32)[None, :]
    angle = (2.0 * math.pi / IMG) * (low * mu).astype(f32)
    twist_col = jnp.broadcast_to(
        jnp.stack([jnp.cos(angle), jnp.sin(angle)], axis=1)[..., None], (8, 2, 16, 128)
    )
    inputs = dict(zip(
        ("table_hi", "table_lo", "up_hi", "up_lo", "down_hi", "down_lo", "sides_hi", "sides_lo"),
        dft512_tables() + wavelet_tables(),
    ))
    inputs = {name: jnp.asarray(table) for name, table in inputs.items()}
    inputs.update(
        table128=jnp.asarray(dft128_table()), twist_row=jnp.asarray(row_twist()),
        twist_col=twist_col, order=jnp.asarray(lane_order()),
        kernels=kernels, coef=coef_dual, sky=sky_image,
        coef_rows=jnp.pad(coef_dual[:, 5:8].reshape(12, 2048), ((0, 4), (0, 0))),
        weights=weights, places=places, live=live, vis_state=vis_state, vis_data=vis_data,
    )
    raw, coeffs, vis_new, totals = step(inputs)
    threshold = 0.5 * totals[0, 0] / (IMG * IMG)
    new_image = jnp.maximum(raw, 0.0)
    new_coef = jnp.clip(coef_dual + coeffs, -threshold, threshold)
    return (new_image, new_coef, vis_new.reshape(1, 1, NV, 4, 2, 32))


def solution(mesh):
    return jax.shard_map(
        local,
        mesh=mesh,
        in_specs=(
            P(("band", "vis"), None),
            P(None, ("band", "vis"), None),
            P("band", "vis", None, None, None, None),
            P("band", "vis", None, None, None, None),
            P("band", "vis", None, None, None, None, None),
            P("band", "vis", None, None),
            P("band", "vis", None),
        ),
        out_specs=(
            P(("band", "vis"), None),
            P(None, ("band", "vis"), None),
            P("band", "vis", None, None, None, None),
        ),
        check_vma=False,
    )
```

profile of v0, /device:TPU:1, one launch (start us, length us, event | category | flops | bytes accessed | tf_op | source)
XLA Modules:
  0.0 125.1 jit_solution(1790078605414064367)
XLA Ops:
  0.7 0.1 broadcast_compare_fusion
  0.8 0.7 fusion.6
  1.5 0.1 copy.23
  1.6 1.1 reshape.277.refs_13_
  2.7 0.0 copy-start.1
  2.7 0.7 compare_select_fusion
  3.4 0.1 slice.30
  3.5 0.1 slice.28
  3.6 0.1 fusion
  3.7 1.3 %compare_convert_fusion.refs_12_ = f32[32,256]{1,0:T(8,128)} fusion(s32[256]{0:T(256)S(1)} %and_select_fusion.3, s32[32]{0:T(128)} %bitcast.25), kind=kLoop, calls=%fused_computation.3 | loop fusion | flops 16384 | bytes 33920 | tf_op jit(solution)/shard_map/convert_element_type | solution.py:576
  5.0 1.7 %reshape.279.refs_14_ = f32[32,256]{1,0:T(8,128)} reshape(f32[1,1,32,4,2,32]{5,4,3,2,1,0:T(2,128)} %param.21) | data formatting | bytes 65536 | tf_op jit(solution)/shard_map/reshape | solution.py:577
  6.7 0.8 select_convert_fusion.refs_10_
  7.4 0.8 broadcast_in_dim.73.refs_11_
  8.2 0.7 broadcast_in_dim.74.refs_17_
  8.9 1.0 slice.22
  10.0 0.7 pad.4.refs_9_
  10.6 0.0 copy-done.1
  10.6 0.0 copy-start
  10.7 107.7 %shard_map.193 = (f32[16,4096]{1,0:T(8,128)}, f32[4,8,2048]{2,1,0:T(8,128)}, f32[32,256]{1,0:T(8,128)}, f32[8,128]{1,0:T(8,128)}) custom-call(bf16[32,256,128]{2,1,0:T(8,128)(2,1)} %bitcast.21, f32[4,8,2048]{2,1,0:T(8,128)} %refs_1_.1, f32[16,4096]{1,0:T(8,128)} %refs_2_.1, bf16[512,256]{1,0:T(8,128)(2,1)} %constant.140.clone.refs_3_, ...), custom_call_target="tpu_custom_call" | custom-call | tf_op jit(solution)/shard_map/pallas_call | solution.py:555
  118.4 1.2 slice.27
  120.2 1.7 %broadcast_maximum_fusion = f32[16,4096]{1,0:T(8,128)} fusion(f32[16,4096]{1,0:T(8,128)} %get-tuple-element.7), kind=kLoop, calls=%fused_computation.2 | loop fusion | flops 65536 | bytes 524288 | tf_op jit(solution)/shard_map/max | solution.py:614
  121.9 1.6 %reshape.280 = f32[1,1,32,4,2,32]{5,4,3,2,1,0:T(2,128)} reshape(f32[32,256]{1,0:T(8,128)} %get-tuple-element.10) | data formatting | bytes 65536 | tf_op jit(solution)/shard_map/reshape | solution.py:616
  123.4 0.0 copy-done
  123.4 1.7 %maximum_minimum_fusion = f32[4,8,2048]{2,1,0:T(8,128)} fusion(f32[4,8,2048]{2,1,0:T(8,128)S(1)} %copy-done, f32[4,8,2048]{2,1,0:T(8,128)} %get-tuple-element.9, f32[]{:T(128)S(6)} %neg.11, f32[]{:T(128)} %bitcast.4), kind=kLoop, calls=%fused_computation | loop fusion | flops 196608 | bytes 786440 | tf_op jit(solution)/shard_map/jit(clip)/min | solution.py:615
  (11 shorter events, 0.1 us)
Async XLA Ops:
  2.7 8.0 %copy-start.1 = (f32[32,256]{1,0:T(8,128)}, f32[32,256]{1,0:T(8,128)S(1)}, u32[]{:S(2)}) copy-start(f32[32,256]{1,0:T(8,128)S(1)} %reshape.277.refs_13_) | copy-start | bytes 98308
  10.6 112.8 %copy-start = (f32[4,8,2048]{2,1,0:T(8,128)S(1)}, f32[4,8,2048]{2,1,0:T(8,128)}, u32[]{:S(2)}) copy-start(f32[4,8,2048]{2,1,0:T(8,128)} %refs_1_.1) | copy-start | bytes 786436
where the time goes:
time: 126 us; the launch traced here: 125 us
  Pallas kernels  108 us (86%)
  local copies, waits for them, and re-layouts  8.94 us (7%)
  other arithmetic  7.11 us (6%)
  between operations  1.37 us (1%)
    pallas_call x1, Pallas kernels, step(): pl.pallas_call(step_kernel, out_shape=(jax.ShapeDtypeStruct((16, IMG), f3...  108 us

commit v1 on v0

--- a/solution.py
+++ b/solution.py
@@ -13,7 +13,6 @@
 NB = 8
 NV = 32
 MESH_ID = pl.DeviceIdType.MESH
-highest = lax.Precision.HIGHEST
 f32 = jnp.float32
 bf16 = jnp.bfloat16
 
@@ -42,15 +41,25 @@
     return halves_of(np.concatenate([np.cos(angle), np.sin(angle)], axis=0))
 
 
-def dft128_table():
+def dft128_tables():
     index = np.arange(128)
     angle = 2.0 * np.pi / 128 * (index[:, None] * index[None, :] % 128)
-    return (np.concatenate([np.cos(angle), np.sin(angle)], axis=1) / IMG).astype(np.float32)
+    return halves_of(np.concatenate([np.cos(angle), np.sin(angle)], axis=1) / IMG)
 
 
 def row_twist():
     angle = 2.0 * np.pi / IMG * (np.arange(32)[:, None] * np.arange(128)[None, :] % IMG)
     return np.stack([np.cos(angle), np.sin(angle)], axis=1).astype(np.float32)
+
+
+def col_twist():
+    low, row = np.arange(8)[None, :, None], np.arange(16)[None, None, :]
+    angle = 2.0 * np.pi / IMG * (low * (16 * np.arange(NV)[:, None, None] + row))
+    return np.stack([np.cos(angle), np.sin(angle)], axis=1).reshape(NV, 2, 128).astype(np.float32)
+
+
+def repeat_table():
+    return np.tile(np.eye(32), (1, 8)).astype(bf16)
 
 
 def wavelet_tables():
@@ -251,16 +260,61 @@
 
     barrier = greet(vis_me, band_me, (following, preceding))
 
-    weights, places, sent_a, got_a = r["weights"], r["places"], r["sent_a"], r["got_a"]
+    to_row = (
+        lax.broadcasted_iota(jnp.int32, (256, 32), 0) // 8
+        == lax.broadcasted_iota(jnp.int32, (256, 32), 1)
+    ).astype(f32).astype(bf16)
+    column = r["rows"][...]
+    facts = jnp.concatenate(
+        [column % 32 * 16 + column // 32 - 256, r["counts"][...], jnp.zeros((3, 32), jnp.int32)],
+        axis=0,
+    ).astype(f32).astype(bf16)
+    facts = dot_nt(to_row, facts)
+    slot_here = lax.broadcasted_iota(jnp.int32, (256, 8), 0) % 8 // 2
+    fact = lax.broadcasted_iota(jnp.int32, (256, 8), 1)
+    place = jnp.sum(jnp.where(fact == slot_here, facts, 0.0), axis=1, keepdims=True)
+    count = jnp.sum(jnp.where(fact == 4, facts, 0.0), axis=1, keepdims=True)
+    places = jnp.broadcast_to(place, (256, 128)).reshape(NV, 8, 128)
+    live = jnp.broadcast_to(count, (256, 32)) > (
+        lax.broadcasted_iota(jnp.int32, (256, 32), 0) % 8 // 2
+    ).astype(f32)
+    live = jnp.where(live, 1.0, 0.0)
+    vis_state = r["vis_state"][...].reshape(256, 32)
+    vis_data = r["vis_data"][...].reshape(256, 32)
+    data_square = jnp.sum(live * vis_data * vis_data)
+
+    weights = dot((live * vis_state).astype(bf16), r["repeat"][...]).reshape(NV, 8, 256)
+    wide_row = lax.broadcasted_iota(jnp.int32, (NV, 8, 256), 1)
+    wide_lane = lax.broadcasted_iota(jnp.int32, (NV, 8, 256), 2)
+    crossed = jnp.where(
+        wide_row % 2 == 0, pltpu.roll(weights, 7, 1), -pltpu.roll(weights, 1, 1)
+    )
+    weights = jnp.where(wide_lane // 32 % 2 == 0, weights, crossed)
+    r["weights"][...] = jnp.where(wide_lane // 64 == wide_row // 2, weights, 0.0).astype(bf16)
+    twist_col = r["twist_col"]
+    eye = (
+        lax.broadcasted_iota(jnp.int32, (128, 128), 0)
+        == lax.broadcasted_iota(jnp.int32, (128, 128), 1)
+    )
+    for c in range(2):
+        one = jnp.broadcast_to(r["twists"][vis_me, c : c + 1, :], (128, 128))
+        one = jnp.sum(jnp.where(eye, one, 0.0), axis=1, keepdims=True)
+        twist_col[:, c] = jnp.broadcast_to(one, (128, 128)).reshape(8, 16, 128)
+
+    sent_a, got_a = r["sent_a"], r["got_a"]
+    coef = staged("coef")
+    for part in range(4):
+        r["coef_rows"][3 * part : 3 * part + 3] = coef[part, 5:8, :]
+    r["coef_rows"][12:16] = jnp.zeros((4, 2048), f32)
     kernels = staged("kernels")
     for q in range(NV):
-        part = dot(weights[q], kernels[q])
+        part = dot(r["weights"][q], kernels[q])
         sent_a[q] = jnp.concatenate([part, places[q]], axis=0).astype(bf16)
     pl.semaphore_wait(barrier, NV + NB)
     launch(sent_a, got_a, r["sem_a"], "vis", NV, vis_me)
     coef_copy = to_neighbour(r["coef_rows"], r["got_coef"], r["sem_coef"], following)
 
-    coef, sky = staged("coef"), staged("sky")
+    sky = staged("sky")
     sides_hi, sides_lo = r["sides_hi"], r["sides_lo"]
     up_hi, up_lo = staged("up_hi"), staged("up_lo")
     coef_copy.wait_recv()
@@ -313,7 +367,7 @@
     launch(sent_c, got_c, r["sem_c"], "vis", NV, vis_me)
     arrived(got_c, r["sem_c"], NV)
 
-    sent_d, got_d, twist_col = r["sent_d"], r["got_d"], r["twist_col"]
+    sent_d, got_d = r["sent_d"], r["got_d"]
     for g in range(4):
         values = []
         for low in range(8):
@@ -328,7 +382,7 @@
     launch(sent_d, got_d, r["sem_d"], "band", NB, band_me)
     arrived(got_d, r["sem_d"], NB)
 
-    mid, table128, twist_row = r["mid"], r["table128"], r["twist_row"]
+    mid, twist_row = r["mid"], r["twist_row"]
     for g in range(4):
         for c in range(2):
             parts = swap_groups(
@@ -336,8 +390,8 @@
             )
             for a in range(8):
                 mid[g * 8 + a, c] = parts[a]
-    lanes = jnp.dot(
-        mid[...].reshape(1024, 128), table128[...], precision=highest, preferred_element_type=f32
+    lanes = by_table(
+        mid[...].reshape(1024, 128), r["lane_hi"][...], r["lane_lo"][...]
     ).reshape(32, 2, 16, 256)
     extrap = r["extrap"]
     for half in range(2):
@@ -351,12 +405,12 @@
         values = small_dft(values, 1.0)
         for n in range(32):
             cols = slice(128 * n, 128 * n + 128)
-            now = raw[rows, cols] - values[n][0]
+            now = jnp.maximum(raw[rows, cols] - values[n][0], 0.0)
             raw[rows, cols] = now
-            extrap[rows, cols] = 2.0 * jnp.maximum(now, 0.0) - sky[rows, cols]
+            extrap[rows, cols] = 2.0 * now - sky[rows, cols]
     image_copy = to_neighbour(extrap.at[pl.ds(0, 8)], r["got_rows"], r["sem_rows"], preceding)
-    out_raw = pltpu.make_async_copy(raw, r["raw"], r["sem_out"].at[0])
-    out_raw.start()
+    out_image = pltpu.make_async_copy(raw, r["image"], r["sem_out"].at[0])
+    out_image.start()
 
     sent_e, got_e = r["sent_e"], r["got_e"]
     for half in range(2):
@@ -372,8 +426,8 @@
             else:
                 mid[a, 0, rows] = re * cosine + im * sine
                 mid[a, 1, rows] = im * cosine - re * sine
-    lanes = jnp.dot(
-        mid[...].reshape(1024, 128), table128[...], precision=highest, preferred_element_type=f32
+    lanes = by_table(
+        mid[...].reshape(1024, 128), r["lane_hi"][...], r["lane_lo"][...]
     ).reshape(32, 2, 16, 256)
     for g in range(4):
         for c in range(2):
@@ -409,8 +463,6 @@
         coeffs[2, :, cols] = block[8:16, :128]
         coeffs[3, :, cols] = block[8:16, 128:]
     abs_total = jnp.sum(jnp.abs(found))
-    out_coeffs = pltpu.make_async_copy(coeffs, r["coeffs"], r["sem_out"].at[1])
-    out_coeffs.start()
     arrived(got_e, r["sem_e"], NB)
 
     sent_f, got_f = r["sent_f"], r["got_f"]
@@ -456,29 +508,23 @@
     tiles = dot(tiles, order[...])
     sent_h[...] = tiles.reshape(NV, 8, 128).astype(bf16)
     launch(sent_h, got_h, r["sem_h"], "vis", NV, vis_me)
-    data_square = jnp.sum(r["live"][...] * r["vis_data"][...] * r["vis_data"][...])
     arrived(got_h, r["sem_h"], NV)
 
-    row = lax.broadcasted_iota(jnp.int32, (8, 256), 0)
-    slot = lax.broadcasted_iota(jnp.int32, (8, 256), 1) // 64
-    on_real = row == 2 * slot
-    on_imag = row == 2 * slot + 1
-    from_real, from_imag = [], []
-    for q in range(NV):
-        product = dot_nt(got_h[q], kernels[q])
-        from_real.append(jnp.sum(jnp.where(on_real, product, 0.0), axis=0, keepdims=True))
-        from_imag.append(jnp.sum(jnp.where(on_imag, product, 0.0), axis=0, keepdims=True))
-    from_real = jnp.concatenate(from_real, axis=0)
-    from_imag = jnp.concatenate(from_imag, axis=0)
-    imag_lane = (lax.broadcasted_iota(jnp.int32, (NV, 256), 1) // 32) % 2 == 1
-    predicted = from_real + jnp.where(
-        imag_lane, pltpu.roll(from_imag, 32, 1), -pltpu.roll(from_imag, 256 - 32, 1)
-    )
-    residual = r["live"][...] * (r["vis_state"][...] + predicted - r["vis_data"][...])
+    products = jnp.stack([dot_nt(got_h[q], kernels[q]) for q in range(NV)])
+    products = jnp.where(wide_lane // 64 == wide_row // 2, products, 0.0)
+    products = products[:, :, 0:128] + products[:, :, 128:256]
+    products = products + pltpu.roll(products, 64, 2)
+    other = pltpu.roll(products, 96, 2)
+    row = lax.broadcasted_iota(jnp.int32, (NV, 8, 128), 1)
+    products = products + jnp.where(
+        row % 2 == 0, -pltpu.roll(other, 7, 1), pltpu.roll(other, 1, 1)
+    )
+    predicted = products.reshape(256, 128)[:, 0:32]
+    residual = live * (vis_state + predicted - vis_data)
     resid_square = jnp.sum(residual * residual)
 
     sent_t, got_t, sent_u, got_u = r["sent_t"], r["got_t"], r["sent_u"], r["got_u"]
-    spot = lax.broadcasted_iota(jnp.int32, (8, 128), 0)
+    spot = lax.broadcasted_iota(jnp.int32, (1, 128), 1)
     sent_t[...] = jnp.where(
         spot == 0, abs_total, jnp.where(spot == 1, resid_square, data_square)
     )
@@ -488,16 +534,23 @@
     launch(sent_u, got_u, r["sem_u"], "band", NB, band_me, same=True)
     arrived(got_u, r["sem_u"], NB)
     totals = jnp.sum(got_u[...], axis=0)
-    r["totals"][...] = totals
-    radius = 0.5 * jnp.sqrt(totals[2:3, :] + 1e-06)
-    size = jnp.sqrt(totals[1:2, :] + 1e-06)
-    factor = 1.0 - jnp.minimum(1.0, radius / size)
-    r["vis_new"][:, 0:128] = residual[:, 0:128] * factor
-    r["vis_new"][:, 128:256] = residual[:, 128:256] * factor
+    abs_total, resid_square, data_square = (
+        jnp.sum(jnp.where(spot == n, totals, 0.0), axis=1, keepdims=True) for n in range(3)
+    )
+    threshold = 0.5 * abs_total / (IMG * IMG)
+    for part in range(4):
+        limit = jnp.broadcast_to(threshold, (8, 2048))
+        coeffs[part] = jnp.maximum(jnp.minimum(coef[part] + coeffs[part], limit), -limit)
+    out_coeffs = pltpu.make_async_copy(coeffs, r["coeffs"], r["sem_out"].at[1])
+    out_coeffs.start()
+    radius = 0.5 * jnp.sqrt(data_square + 1e-06)
+    size = jnp.sqrt(resid_square + 1e-06)
+    factor = jnp.broadcast_to(1.0 - jnp.minimum(1.0, radius / size), (256, 32))
+    r["vis_new"][...] = (residual * factor).reshape(NV, 4, 2, 32)
 
     for copy in (coef_copy, image_copy):
         copy.wait_send()
-    out_raw.wait()
+    out_image.wait()
     out_coeffs.wait()
     for name, landed, count in (
         ("a", got_a, NV), ("b", got_b, NV), ("c", got_c, NV), ("d", got_d, NB),
@@ -509,10 +562,10 @@
 
 STAGED = ["kernels", "coef", "sky", "up_hi", "up_lo", "table_hi", "table_lo", "down_hi", "down_lo"]
 INPUTS = STAGED + [
-    "coef_rows", "weights", "places", "live", "vis_state", "vis_data",
-    "table128", "twist_row", "twist_col", "order", "sides_hi", "sides_lo",
+    "vis_state", "vis_data", "rows", "counts", "repeat", "lane_hi", "lane_lo",
+    "twist_row", "twists", "order", "sides_hi", "sides_lo",
 ]
-OUTPUTS = ["raw", "coeffs", "vis_new", "totals"]
+OUTPUTS = ["image", "coeffs", "vis_new"]
 VIS_TILE = (NV, 2, 16, 128)
 BAND_TILE = (NB, 2, 16, 512)
 SCRATCH = dict(
@@ -533,8 +586,9 @@
     sent_f=(VIS_TILE, f32), got_f=(VIS_TILE, f32),
     sent_g=(VIS_TILE, bf16), got_g=(VIS_TILE, bf16),
     sent_h=((NV, 8, 128), bf16), got_h=((NV, 8, 128), bf16),
-    sent_t=((8, 128), f32), got_t=((NV, 8, 128), f32),
-    sent_u=((8, 128), f32), got_u=((NB, 8, 128), f32),
+    sent_t=((1, 128), f32), got_t=((NV, 1, 128), f32),
+    sent_u=((1, 128), f32), got_u=((NB, 1, 128), f32),
+    weights=((NV, 8, 256), bf16), twist_col=((8, 2, 16, 128), f32), coef_rows=((16, 2048), f32),
     got_coef=((16, 2048), f32), got_rows=((8, IMG), f32),
     raw_here=((16, IMG), f32), extrap=((16, IMG), f32), coeffs_here=((4, 8, 2048), f32),
     onehot=((256, 512), bf16), mid=((32, 2, 16, 128), f32),
@@ -557,11 +611,10 @@
         out_shape=(
             jax.ShapeDtypeStruct((16, IMG), f32),
             jax.ShapeDtypeStruct((4, 8, 2048), f32),
-            jax.ShapeDtypeStruct((NV, 256), f32),
-            jax.ShapeDtypeStruct((8, 128), f32),
+            jax.ShapeDtypeStruct((NV, 4, 2, 32), f32),
         ),
         in_specs=[anywhere if name in STAGED else vmem for name in INPUTS],
-        out_specs=(anywhere, anywhere, vmem, vmem),
+        out_specs=(anywhere, anywhere, vmem),
         scratch_shapes=scratch,
         compiler_params=pltpu.CompilerParams(
             collective_id=0, has_side_effects=True, vmem_limit_bytes=56 * 2**20
@@ -570,50 +623,26 @@
 
 
 def local(sky_image, coef_dual, vis_dual, visibilities, kernel_blocks, tile_rows, tile_counts):
-    kernels = kernel_blocks.reshape(NV, 256, 128)
-    rows_here = tile_rows.reshape(NV, 4)
-    counts = tile_counts.reshape(NV, 1)
-    live = (jnp.arange(256, dtype=jnp.int32)[None, :] // 64 < counts).astype(f32)
-    vis_data = visibilities.reshape(NV, 256)
-    vis_state = vis_dual.reshape(NV, 256)
-
-    wb = live * vis_state
-    lane = jnp.arange(256, dtype=jnp.int32)
-    imag_lane = (lane // 32) % 2 == 1
-    crossed = jnp.where(imag_lane, -jnp.roll(wb, 32, axis=1), jnp.roll(wb, -32, axis=1))
-    slot_row = jnp.arange(8, dtype=jnp.int32)
-    same = (slot_row[:, None] // 2 == lane[None, :] // 64)[None]
-    chosen = jnp.where((slot_row % 2 == 1)[None, :, None], crossed[:, None, :], wb[:, None, :])
-    weights = jnp.where(same, chosen, 0.0).astype(bf16)
-
-    place = (rows_here % 32) * 16 + rows_here // 32 - 256
-    places = jnp.broadcast_to(
-        jnp.repeat(place.astype(f32), 2, axis=1)[:, :, None], (NV, 8, 128)
-    )
-
-    low = jnp.arange(8, dtype=jnp.int32)[:, None]
-    mu = lax.axis_index("vis") * 16 + jnp.arange(16, dtype=jnp.int32)[None, :]
-    angle = (2.0 * math.pi / IMG) * (low * mu).astype(f32)
-    twist_col = jnp.broadcast_to(
-        jnp.stack([jnp.cos(angle), jnp.sin(angle)], axis=1)[..., None], (8, 2, 16, 128)
-    )
-    inputs = dict(zip(
-        ("table_hi", "table_lo", "up_hi", "up_lo", "down_hi", "down_lo", "sides_hi", "sides_lo"),
-        dft512_tables() + wavelet_tables(),
-    ))
+    names = (
+        "table_hi", "table_lo", "lane_hi", "lane_lo",
+        "up_hi", "up_lo", "down_hi", "down_lo", "sides_hi", "sides_lo",
+    )
+    inputs = dict(zip(names, dft512_tables() + dft128_tables() + wavelet_tables()))
+    inputs.update(
+        twist_row=row_twist(), twists=col_twist(), order=lane_order(), repeat=repeat_table()
+    )
     inputs = {name: jnp.asarray(table) for name, table in inputs.items()}
     inputs.update(
-        table128=jnp.asarray(dft128_table()), twist_row=jnp.asarray(row_twist()),
-        twist_col=twist_col, order=jnp.asarray(lane_order()),
-        kernels=kernels, coef=coef_dual, sky=sky_image,
-        coef_rows=jnp.pad(coef_dual[:, 5:8].reshape(12, 2048), ((0, 4), (0, 0))),
-        weights=weights, places=places, live=live, vis_state=vis_state, vis_data=vis_data,
-    )
-    raw, coeffs, vis_new, totals = step(inputs)
-    threshold = 0.5 * totals[0, 0] / (IMG * IMG)
-    new_image = jnp.maximum(raw, 0.0)
-    new_coef = jnp.clip(coef_dual + coeffs, -threshold, threshold)
-    return (new_image, new_coef, vis_new.reshape(1, 1, NV, 4, 2, 32))
+        kernels=kernel_blocks.reshape(NV, 256, 128),
+        coef=coef_dual,
+        sky=sky_image,
+        vis_state=vis_dual.reshape(NV, 4, 2, 32),
+        vis_data=visibilities.reshape(NV, 4, 2, 32),
+        rows=tile_rows.reshape(NV, 4).T,
+        counts=tile_counts.reshape(1, NV),
+    )
+    image, coeffs, vis_new = step(inputs)
+    return (image, coeffs, vis_new.reshape(1, 1, NV, 4, 2, 32))
 
 
 def solution(mesh):

time: 126 us -> 110 us (0.87)
  other arithmetic: 7.11 us -> 0 us
  local copies, waits for them, and re-layouts: 8.94 us -> 4.91 us
  Pallas kernels: 108 us -> 105 us
    unnamed x4 -> x3, local copies, waits for them, and re-layouts: 0.01 us -> 4.91 us
    reshape x4 -> x0, local copies, waits for them, and re-layouts: 4.37 us -> none  [the longest x1 1.68 us: local(): vis_data = visibilities.reshape(NV, 256)]
    pallas_call x1, Pallas kernels: 108 us -> 105 us  [step(): pl.pallas_call(step_kernel, out_shape=(jax.ShapeDtypeStruct((16, IMG), f3...]
    convert_element_type x3 -> x0, other arithmetic: 2.78 us -> none  [the longest x1 1.33 us: local(): (jnp.arange(256, dtype=jnp.int32)[None, :] // 64 < counts).astype(f32)]
    slice x5 -> x0, local copies, waits for them, and re-layouts: 2.32 us -> none  [the longest x1 1.19 us: local(): threshold = 0.5 * totals[0, 0] / (IMG * IMG)]
    min x1 -> x0, other arithmetic: 1.68 us -> none  [local(): new_coef = jnp.clip(coef_dual + coeffs, -threshold, threshold)]
    max x1 -> x0, other arithmetic: 1.67 us -> none  [local(): new_image = jnp.maximum(raw, 0.0)]
    broadcast_in_dim x4 -> x0, local copies, waits for them, and re-layouts: 1.57 us -> none  [the longest x2 0.83 us: local(): jnp.broadcast_to(jnp.repeat(place.astype(f32), 2, axis=1)[:, :, None], (N...]
where the time goes in v1:
time: 110 us
  Pallas kernels  105 us (95%)
  local copies, waits for them, and re-layouts  4.91 us (4%)
    pallas_call x1, Pallas kernels, step(): pl.pallas_call(step_kernel, out_shape=(jax.ShapeDtypeStruct((16, IMG), f3...  105 us
    unnamed x3, local copies, waits for them, and re-layouts  4.91 us

profile of v1, /device:TPU:1, one launch (start us, length us, event | category | flops | bytes accessed | tf_op | source)
XLA Modules:
  0.0 110.3 jit_solution(3565300093458067762)
XLA Ops:
  0.6 104.7 %shard_map.220 = (f32[16,4096]{1,0:T(8,128)}, f32[4,8,2048]{2,1,0:T(8,128)}, f32[32,4,2,32]{3,2,1,0:T(2,128)}) custom-call(bf16[32,256,128]{2,1,0:T(8,128)(2,1)} %bitcast.8, f32[4,8,2048]{2,1,0:T(8,128)} %refs_1_.1, f32[16,4096]{1,0:T(8,128)} %refs_2_.1, bf16[512,256]{1,0:T(8,128)(2,1)} %constant.32.clone.refs_3_, bf16[512,256]{1,0:T(8,128)(2,1)} %constant.33.clone.refs_4_, ...), custom_call_target="tpu_custom_call" | custom-call | tf_op jit(solution)/shard_map/pallas_call | solution.py:609
  105.4 1.7 %copy.27 = f32[16,4096]{1,0:T(8,128)} copy(f32[16,4096]{1,0:T(8,128)} %get-tuple-element.12) | data formatting | bytes 524288
  107.1 1.7 %copy.28 = f32[4,8,2048]{2,1,0:T(8,128)} copy(f32[4,8,2048]{2,1,0:T(8,128)} %get-tuple-element.13) | data formatting | bytes 524288
  108.7 1.6 %copy.29 = f32[1,1,32,4,2,32]{5,4,3,2,1,0:T(2,128)} copy(f32[1,1,32,4,2,32]{5,4,3,2,1,0:T(2,128)} %bitcast.11) | data formatting | bytes 65536

commit v2 on v1

--- a/solution.py
+++ b/solution.py
@@ -36,7 +36,7 @@
 
 
 def dft512_tables():
-    index = np.arange(512)
+    index = np.arange(512).reshape(32, 2, 8).transpose(1, 0, 2).reshape(512)
     angle = 2.0 * np.pi / 512 * (index[:, None] * index[None, :] % 512)
     return halves_of(np.concatenate([np.cos(angle), np.sin(angle)], axis=0))
 
@@ -90,7 +90,7 @@
 def lane_order():
     place = np.zeros((128, 128), np.float32)
     for t in range(128):
-        place[(t % 8) * 16 + t // 8, t] = 1.0
+        place[t // 64 * 64 + (t % 8) * 8 + t // 8 % 8, t] = 1.0
     return place.astype(bf16)
 
 
@@ -199,14 +199,18 @@
     return barrier
 
 
-def launch(sent, landed, sems, axis, count, me, same=False):
+def launch(r, name, part, axis, count, me, same=False):
+    sent, landed, sems = r["sent_" + name], r["got_" + name].at[part], r["sem_" + name]
+    if not same:
+        sent = sent.at[part]
+
     def body(d, carry):
         peer = me ^ d
         pltpu.make_async_remote_copy(
             src_ref=sent if same else sent.at[peer],
             dst_ref=landed.at[me],
-            send_sem=sems.at[0],
-            recv_sem=sems.at[1],
+            send_sem=sems.at[2 * part],
+            recv_sem=sems.at[2 * part + 1],
             device_id={axis: peer},
             device_id_type=MESH_ID,
         ).start()
@@ -229,14 +233,15 @@
     return copy
 
 
-def arrived(landed, sems, count):
-    part = landed.at[pl.ds(0, count - 1)]
-    pltpu.make_async_copy(part, part, sems.at[1]).wait()
-
-
-def drained(landed, sems, count):
-    part = landed.at[pl.ds(0, count - 1)]
-    pltpu.make_async_copy(part, part, sems.at[0]).wait()
+def finish(r, name, part, count, side):
+    landed = r["got_" + name].at[part]
+    landed = landed.at[pl.ds(0, count - 1)]
+    pltpu.make_async_copy(landed, landed, r["sem_" + name].at[2 * part + side]).wait()
+
+
+def arrived(r, name, part, count):
+    finish(r, name, part, count, 1)
+    return r["got_" + name].at[part]
 
 
 def step_kernel(*refs):
@@ -301,7 +306,7 @@
         one = jnp.sum(jnp.where(eye, one, 0.0), axis=1, keepdims=True)
         twist_col[:, c] = jnp.broadcast_to(one, (128, 128)).reshape(8, 16, 128)
 
-    sent_a, got_a = r["sent_a"], r["got_a"]
+    sent_a = r["sent_a"].at[0]
     coef = staged("coef")
     for part in range(4):
         r["coef_rows"][3 * part : 3 * part + 3] = coef[part, 5:8, :]
@@ -311,7 +316,7 @@
         part = dot(r["weights"][q], kernels[q])
         sent_a[q] = jnp.concatenate([part, places[q]], axis=0).astype(bf16)
     pl.semaphore_wait(barrier, NV + NB)
-    launch(sent_a, got_a, r["sem_a"], "vis", NV, vis_me)
+    launch(r, "a", 0, "vis", NV, vis_me)
     coef_copy = to_neighbour(r["coef_rows"], r["got_coef"], r["sem_coef"], following)
 
     sky = staged("sky")
@@ -335,9 +340,9 @@
     for n in range(16):
         cols = slice(256 * n, 256 * n + 256)
         raw[:, cols] = sky[:, cols] - smooth[16 * n : 16 * n + 16]
-    arrived(got_a, r["sem_a"], NV)
-
-    order, onehot, sent_b, got_b = r["order"], r["onehot"], r["sent_b"], r["got_b"]
+    got_a = arrived(r, "a", 0, NV)
+
+    order, onehot = r["order"], r["onehot"]
     contrib = got_a[:, 0:8, :].astype(f32).reshape(256, 128).astype(bf16)
     where_to = got_a[:, 8:16, :].astype(f32).reshape(256, 128)
     lane = lax.broadcasted_iota(jnp.int32, (256, 128), 1).astype(f32)
@@ -347,59 +352,84 @@
         onehot[:, 128 * g : 128 * g + 128] = hots[g].astype(bf16)
     real_hots = [jnp.where(is_imag, 0.0, h).astype(bf16) for h in hots]
     imag_hots = [jnp.where(is_imag, h, 0.0).astype(bf16) for h in hots]
+    hots = jnp.concatenate(real_hots + imag_hots, axis=1)
     turned = dot_nt(order[...], contrib).astype(bf16)
-    for c, some in ((0, real_hots), (1, imag_hots)):
+    for part in range(2):
+        grid = dot(turned[64 * part : 64 * part + 64], hots)
+        for c in range(2):
+            for g in range(4):
+                cols = slice(512 * c + 128 * g, 512 * c + 128 * g + 128)
+                for low in range(8):
+                    r["sent_b"][part, low * 4 + g, c] = grid[
+                        8 * low : 8 * low + 8, cols
+                    ].astype(bf16)
+        launch(r, "b", part, "vis", NV, vis_me)
+
+    table_hi, table_lo = staged("table_hi"), staged("table_lo")
+
+    def spread_of(landed):
+        return jnp.concatenate(
+            [landed[:, 0].reshape(256, 128), landed[:, 1].reshape(256, 128)], axis=1
+        )
+
+    first = spread_of(arrived(r, "b", 0, NV))
+    ahead = dot(table_hi[:, 0:256], first) + dot(table_lo[:, 0:256], first)
+    second = spread_of(arrived(r, "b", 1, NV))
+    for part in range(2):
+        both = []
+        for side in range(2):
+            rows = slice(512 * side + 256 * part, 512 * side + 256 * part + 256)
+            both.append(
+                ahead[rows] + dot(table_hi[rows, 256:512], second)
+                + dot(table_lo[rows, 256:512], second)
+            )
+        re = both[0][:, :128] - both[1][:, 128:]
+        im = both[1][:, :128] + both[0][:, 128:]
+        r["sent_c"][part, :, 0] = re.reshape(NV, 8, 128).astype(bf16)
+        r["sent_c"][part, :, 1] = im.reshape(NV, 8, 128).astype(bf16)
+        launch(r, "c", part, "vis", NV, vis_me)
+
+    sent_d = r["sent_d"]
+    for part in range(2):
+        got_c = arrived(r, "c", part, NV)
+        rows = slice(8 * part, 8 * part + 8)
         for g in range(4):
-            grid = dot(turned, some[g]).astype(bf16)
+            values = []
             for low in range(8):
-                sent_b[low * 4 + g, c] = grid[16 * low : 16 * low + 16]
-    launch(sent_b, got_b, r["sem_b"], "vis", NV, vis_me)
-    table_hi, table_lo = staged("table_hi"), staged("table_lo")
-    arrived(got_b, r["sem_b"], NV)
-
-    sent_c, got_c = r["sent_c"], r["got_c"]
-    spread = jnp.concatenate(
-        [got_b[:, 0].reshape(512, 128), got_b[:, 1].reshape(512, 128)], axis=1
-    )
-    both = dot(table_hi[...], spread) + dot(table_lo[...], spread)
-    sent_c[:, 0] = (both[:512, :128] - both[512:, 128:]).astype(bf16).reshape(NV, 16, 128)
-    sent_c[:, 1] = (both[512:, :128] + both[:512, 128:]).astype(bf16).reshape(NV, 16, 128)
-    launch(sent_c, got_c, r["sem_c"], "vis", NV, vis_me)
-    arrived(got_c, r["sem_c"], NV)
-
-    sent_d, got_d = r["sent_d"], r["got_d"]
-    for g in range(4):
-        values = []
-        for low in range(8):
-            re = got_c[low * 4 + g, 0].astype(f32)
-            im = got_c[low * 4 + g, 1].astype(f32)
-            cosine, sine = twist_col[low, 0], twist_col[low, 1]
-            values.append((re * cosine - im * sine, re * sine + im * cosine))
-        values = small_dft(values, 1.0)
-        for b in range(NB):
+                re = got_c[low * 4 + g, 0].astype(f32)
+                im = got_c[low * 4 + g, 1].astype(f32)
+                cosine, sine = twist_col[low, 0, rows], twist_col[low, 1, rows]
+                values.append((re * cosine - im * sine, re * sine + im * cosine))
+            values = small_dft(values, 1.0)
+            for b in range(NB):
+                for c in range(2):
+                    sent_d[part, b, c, :, 128 * g : 128 * g + 128] = values[b][c].astype(
+                        sent_d.dtype
+                    )
+        launch(r, "d", part, "band", NB, band_me)
+
+    mid, twist_row, extrap, sent_e = r["mid"], r["twist_row"], r["extrap"], r["sent_e"]
+
+    def lane_product(part):
+        return by_table(
+            mid[part].reshape(512, 128), r["lane_hi"][...], r["lane_lo"][...]
+        ).reshape(32, 2, 8, 256)
+
+    for part in range(2):
+        rows = slice(8 * part, 8 * part + 8)
+        got_d = arrived(r, "d", part, NB)
+        for g in range(4):
             for c in range(2):
-                sent_d[b, c, :, 128 * g : 128 * g + 128] = values[b][c].astype(sent_d.dtype)
-    launch(sent_d, got_d, r["sem_d"], "band", NB, band_me)
-    arrived(got_d, r["sem_d"], NB)
-
-    mid, twist_row = r["mid"], r["twist_row"]
-    for g in range(4):
-        for c in range(2):
-            parts = swap_groups(
-                [got_d[b, c, :, 128 * g : 128 * g + 128].astype(f32) for b in range(NB)]
-            )
-            for a in range(8):
-                mid[g * 8 + a, c] = parts[a]
-    lanes = by_table(
-        mid[...].reshape(1024, 128), r["lane_hi"][...], r["lane_lo"][...]
-    ).reshape(32, 2, 16, 256)
-    extrap = r["extrap"]
-    for half in range(2):
-        rows = slice(8 * half, 8 * half + 8)
+                parts = swap_groups(
+                    [got_d[b, c, :, 128 * g : 128 * g + 128].astype(f32) for b in range(NB)]
+                )
+                for a in range(8):
+                    mid[part, g * 8 + a, c] = parts[a]
+        lanes = lane_product(part)
         values = []
         for a in range(32):
-            re = lanes[a, 0, rows, :128] - lanes[a, 1, rows, 128:]
-            im = lanes[a, 0, rows, 128:] + lanes[a, 1, rows, :128]
+            re = lanes[a, 0, :, :128] - lanes[a, 1, :, 128:]
+            im = lanes[a, 0, :, 128:] + lanes[a, 1, :, :128]
             cosine, sine = twist_row[a, 0:1], twist_row[a, 1:2]
             values.append((re * cosine - im * sine, re * sine + im * cosine))
         values = small_dft(values, 1.0)
@@ -407,45 +437,58 @@
             cols = slice(128 * n, 128 * n + 128)
             now = jnp.maximum(raw[rows, cols] - values[n][0], 0.0)
             raw[rows, cols] = now
-            extrap[rows, cols] = 2.0 * now - sky[rows, cols]
-    image_copy = to_neighbour(extrap.at[pl.ds(0, 8)], r["got_rows"], r["sem_rows"], preceding)
-    out_image = pltpu.make_async_copy(raw, r["image"], r["sem_out"].at[0])
-    out_image.start()
-
-    sent_e, got_e = r["sent_e"], r["got_e"]
-    for half in range(2):
-        rows = slice(8 * half, 8 * half + 8)
-        values = [(extrap[rows, 128 * n : 128 * n + 128], None) for n in range(32)]
+            extrap[part, :, cols] = 2.0 * now - sky[rows, cols]
+        if part == 0:
+            image_copy = to_neighbour(extrap.at[0], r["got_rows"], r["sem_rows"], preceding)
+        values = [(extrap[part, :, 128 * n : 128 * n + 128], None) for n in range(32)]
         values = small_dft(values, -1.0)
         for a in range(32):
             re, im = values[a]
             cosine, sine = twist_row[a, 0:1], twist_row[a, 1:2]
             if im is None:
-                mid[a, 0, rows] = re * cosine
-                mid[a, 1, rows] = -re * sine
+                mid[part, a, 0] = re * cosine
+                mid[part, a, 1] = -re * sine
             else:
-                mid[a, 0, rows] = re * cosine + im * sine
-                mid[a, 1, rows] = im * cosine - re * sine
-    lanes = by_table(
-        mid[...].reshape(1024, 128), r["lane_hi"][...], r["lane_lo"][...]
-    ).reshape(32, 2, 16, 256)
-    for g in range(4):
-        for c in range(2):
-            parts = []
-            for a in range(8):
-                re, im = lanes[g * 8 + a, 0], lanes[g * 8 + a, 1]
-                if c == 0:
-                    parts.append(re[:, :128] + im[:, 128:])
-                else:
-                    parts.append(im[:, :128] - re[:, 128:])
-            parts = swap_groups(parts)
+                mid[part, a, 0] = re * cosine + im * sine
+                mid[part, a, 1] = im * cosine - re * sine
+        lanes = lane_product(part)
+        for g in range(4):
+            for c in range(2):
+                parts = []
+                for a in range(8):
+                    re, im = lanes[g * 8 + a, 0], lanes[g * 8 + a, 1]
+                    if c == 0:
+                        parts.append(re[:, :128] + im[:, 128:])
+                    else:
+                        parts.append(im[:, :128] - re[:, 128:])
+                parts = swap_groups(parts)
+                for b in range(NB):
+                    sent_e[part, b, c, :, 128 * g : 128 * g + 128] = parts[b]
+        launch(r, "e", part, "band", NB, band_me)
+    out_image = pltpu.make_async_copy(raw, r["image"], r["sem_out"].at[0])
+    out_image.start()
+
+    sent_f = r["sent_f"]
+    for part in range(2):
+        got_e = arrived(r, "e", part, NB)
+        rows = slice(8 * part, 8 * part + 8)
+        for g in range(4):
+            values = []
             for b in range(NB):
-                sent_e[b, c, :, 128 * g : 128 * g + 128] = parts[b].astype(sent_e.dtype)
-    launch(sent_e, got_e, r["sem_e"], "band", NB, band_me)
+                values.append(
+                    tuple(got_e[b, c, :, 128 * g : 128 * g + 128] for c in range(2))
+                )
+            values = small_dft(values, -1.0)
+            for low in range(8):
+                re, im = values[low]
+                cosine, sine = twist_col[low, 0, rows], twist_col[low, 1, rows]
+                sent_f[part, low * 4 + g, 0] = (re * cosine + im * sine).astype(sent_f.dtype)
+                sent_f[part, low * 4 + g, 1] = (im * cosine - re * sine).astype(sent_f.dtype)
+        launch(r, "f", part, "vis", NV, vis_me)
 
     down_hi, down_lo = staged("down_hi"), staged("down_lo")
     image_copy.wait_recv()
-    fields = jnp.concatenate([extrap[...], r["got_rows"][...]], axis=0)
+    fields = jnp.concatenate([extrap[0], extrap[1], r["got_rows"][...]], axis=0)
     fields = table_by(sides_hi[32:48, 0:24], sides_lo[32:48, 0:24], fields)
     stack = []
     for n in range(16):
@@ -463,52 +506,43 @@
         coeffs[2, :, cols] = block[8:16, :128]
         coeffs[3, :, cols] = block[8:16, 128:]
     abs_total = jnp.sum(jnp.abs(found))
-    arrived(got_e, r["sem_e"], NB)
-
-    sent_f, got_f = r["sent_f"], r["got_f"]
-    for g in range(4):
-        values = []
-        for b in range(NB):
-            values.append(
-                tuple(
-                    got_e[b, c, :, 128 * g : 128 * g + 128].astype(f32) for c in range(2)
-                )
-            )
-        values = small_dft(values, -1.0)
-        for low in range(8):
-            re, im = values[low]
-            cosine, sine = twist_col[low, 0], twist_col[low, 1]
-            sent_f[low * 4 + g, 0] = (re * cosine + im * sine).astype(sent_f.dtype)
-            sent_f[low * 4 + g, 1] = (im * cosine - re * sine).astype(sent_f.dtype)
-    launch(sent_f, got_f, r["sem_f"], "vis", NV, vis_me)
-    arrived(got_f, r["sem_f"], NV)
-
-    sent_g, got_g = r["sent_g"], r["got_g"]
-    spread = jnp.concatenate(
-        [got_f[:, 0].reshape(512, 128), got_f[:, 1].reshape(512, 128)], axis=1
-    )
-    if spread.dtype == f32:
-        both = table_by(table_hi[...], table_lo[...], spread)
-    else:
-        both = dot(table_hi[...], spread) + dot(table_lo[...], spread)
-    sent_g[:, 0] = (both[:512, :128] + both[512:, 128:]).astype(bf16).reshape(NV, 16, 128)
-    sent_g[:, 1] = (both[:512, 128:] - both[512:, :128]).astype(bf16).reshape(NV, 16, 128)
-    launch(sent_g, got_g, r["sem_g"], "vis", NV, vis_me)
-    arrived(got_g, r["sem_g"], NV)
-
-    sent_h, got_h = r["sent_h"], r["got_h"]
-    picked = []
-    for c in range(2):
-        total = 0.0
-        for g in range(4):
-            piece = jnp.concatenate([got_g[low * 4 + g, c] for low in range(8)], axis=0)
-            total = total + dot_nt(onehot[:, 128 * g : 128 * g + 128], piece)
-        picked.append(total)
+
+    def through(rows, cols, spread):
+        if spread.dtype == f32:
+            return table_by(table_hi[rows, cols], table_lo[rows, cols], spread)
+        return dot(table_hi[rows, cols], spread) + dot(table_lo[rows, cols], spread)
+
+    first = spread_of(arrived(r, "f", 0, NV))
+    ahead = through(slice(0, 1024), slice(0, 256), first)
+    second = spread_of(arrived(r, "f", 1, NV))
+    for part in range(2):
+        both = []
+        for side in range(2):
+            rows = slice(512 * side + 256 * part, 512 * side + 256 * part + 256)
+            both.append(ahead[rows] + through(rows, slice(256, 512), second))
+        re = both[0][:, :128] + both[1][:, 128:]
+        im = both[0][:, 128:] - both[1][:, :128]
+        r["sent_g"][part, :, 0] = re.reshape(NV, 8, 128).astype(bf16)
+        r["sent_g"][part, :, 1] = im.reshape(NV, 8, 128).astype(bf16)
+        launch(r, "g", part, "vis", NV, vis_me)
+
+    picked = [[], []]
+    for part in range(2):
+        got_g = arrived(r, "g", part, NV)
+        for c in range(2):
+            total = 0.0
+            for g in range(4):
+                piece = jnp.concatenate(
+                    [got_g[low * 4 + g, c].astype(f32) for low in range(8)], axis=0
+                ).astype(bf16)
+                total = total + dot_nt(onehot[:, 128 * g : 128 * g + 128], piece)
+            picked[c].append(total)
+    picked = [jnp.concatenate(p, axis=1) for p in picked]
     tiles = jnp.where(is_imag, picked[1], picked[0]).astype(bf16)
     tiles = dot(tiles, order[...])
-    sent_h[...] = tiles.reshape(NV, 8, 128).astype(bf16)
-    launch(sent_h, got_h, r["sem_h"], "vis", NV, vis_me)
-    arrived(got_h, r["sem_h"], NV)
+    r["sent_h"][0] = tiles.reshape(NV, 8, 128).astype(bf16)
+    launch(r, "h", 0, "vis", NV, vis_me)
+    got_h = arrived(r, "h", 0, NV)
 
     products = jnp.stack([dot_nt(got_h[q], kernels[q]) for q in range(NV)])
     products = jnp.where(wide_lane // 64 == wide_row // 2, products, 0.0)
@@ -523,17 +557,15 @@
     residual = live * (vis_state + predicted - vis_data)
     resid_square = jnp.sum(residual * residual)
 
-    sent_t, got_t, sent_u, got_u = r["sent_t"], r["got_t"], r["sent_u"], r["got_u"]
+    sent_t, sent_u = r["sent_t"], r["sent_u"]
     spot = lax.broadcasted_iota(jnp.int32, (1, 128), 1)
     sent_t[...] = jnp.where(
         spot == 0, abs_total, jnp.where(spot == 1, resid_square, data_square)
     )
-    launch(sent_t, got_t, r["sem_t"], "vis", NV, vis_me, same=True)
-    arrived(got_t, r["sem_t"], NV)
-    sent_u[...] = jnp.sum(got_t[...], axis=0)
-    launch(sent_u, got_u, r["sem_u"], "band", NB, band_me, same=True)
-    arrived(got_u, r["sem_u"], NB)
-    totals = jnp.sum(got_u[...], axis=0)
+    launch(r, "t", 0, "vis", NV, vis_me, same=True)
+    sent_u[...] = jnp.sum(arrived(r, "t", 0, NV)[...], axis=0)
+    launch(r, "u", 0, "band", NB, band_me, same=True)
+    totals = jnp.sum(arrived(r, "u", 0, NB)[...], axis=0)
     abs_total, resid_square, data_square = (
         jnp.sum(jnp.where(spot == n, totals, 0.0), axis=1, keepdims=True) for n in range(3)
     )
@@ -552,12 +584,9 @@
         copy.wait_send()
     out_image.wait()
     out_coeffs.wait()
-    for name, landed, count in (
-        ("a", got_a, NV), ("b", got_b, NV), ("c", got_c, NV), ("d", got_d, NB),
-        ("e", got_e, NB), ("f", got_f, NV), ("g", got_g, NV), ("h", got_h, NV),
-        ("t", got_t, NV), ("u", got_u, NB),
-    ):
-        drained(landed, r["sem_" + name], count)
+    for name in "abcdefghtu":
+        for part in range(2 if name in "bcdefg" else 1):
+            finish(r, name, part, NB if name in "deu" else NV, 0)
 
 
 STAGED = ["kernels", "coef", "sky", "up_hi", "up_lo", "table_hi", "table_lo", "down_hi", "down_lo"]
@@ -566,8 +595,8 @@
     "twist_row", "twists", "order", "sides_hi", "sides_lo",
 ]
 OUTPUTS = ["image", "coeffs", "vis_new"]
-VIS_TILE = (NV, 2, 16, 128)
-BAND_TILE = (NB, 2, 16, 512)
+VIS_TILE = (2, NV, 2, 8, 128)
+BAND_TILE = (2, NB, 2, 8, 512)
 SCRATCH = dict(
     here_kernels=((NV, 256, 128), bf16),
     here_coef=((4, 8, 2048), f32),
@@ -578,21 +607,21 @@
     here_table_lo=((1024, 512), bf16),
     here_down_hi=((384, 256), bf16),
     here_down_lo=((384, 256), bf16),
-    sent_a=((NV, 16, 128), bf16), got_a=((NV, 16, 128), bf16),
+    sent_a=((1, NV, 16, 128), bf16), got_a=((1, NV, 16, 128), bf16),
     sent_b=(VIS_TILE, bf16), got_b=(VIS_TILE, bf16),
     sent_c=(VIS_TILE, bf16), got_c=(VIS_TILE, bf16),
     sent_d=(BAND_TILE, bf16), got_d=(BAND_TILE, bf16),
     sent_e=(BAND_TILE, f32), got_e=(BAND_TILE, f32),
     sent_f=(VIS_TILE, f32), got_f=(VIS_TILE, f32),
     sent_g=(VIS_TILE, bf16), got_g=(VIS_TILE, bf16),
-    sent_h=((NV, 8, 128), bf16), got_h=((NV, 8, 128), bf16),
-    sent_t=((1, 128), f32), got_t=((NV, 1, 128), f32),
-    sent_u=((1, 128), f32), got_u=((NB, 1, 128), f32),
+    sent_h=((1, NV, 8, 128), bf16), got_h=((1, NV, 8, 128), bf16),
+    sent_t=((1, 128), f32), got_t=((1, NV, 1, 128), f32),
+    sent_u=((1, 128), f32), got_u=((1, NB, 1, 128), f32),
     weights=((NV, 8, 256), bf16), twist_col=((8, 2, 16, 128), f32), coef_rows=((16, 2048), f32),
     got_coef=((16, 2048), f32), got_rows=((8, IMG), f32),
-    raw_here=((16, IMG), f32), extrap=((16, IMG), f32), coeffs_here=((4, 8, 2048), f32),
-    onehot=((256, 512), bf16), mid=((32, 2, 16, 128), f32),
-    **{"sem_" + n: 2 for n in list("abcdefghtu") + ["coef", "rows", "out"]},
+    raw_here=((16, IMG), f32), extrap=((2, 8, IMG), f32), coeffs_here=((4, 8, 2048), f32),
+    onehot=((256, 512), bf16), mid=((2, 32, 2, 8, 128), f32),
+    **{"sem_" + n: 4 for n in list("abcdefghtu") + ["coef", "rows", "out"]},
     sem_in=len(STAGED),
 )
 

time: 110 us -> 105 us (0.955)
  Pallas kernels: 105 us -> 99.6 us
    pallas_call x1, Pallas kernels: 105 us -> 99.6 us  [step(): pl.pallas_call(step_kernel, out_shape=(jax.ShapeDtypeStruct((16, IMG), f3...]
where the time goes in v2:
time: 105 us
  Pallas kernels  99.6 us (95%)
  local copies, waits for them, and re-layouts  4.91 us (5%)
    pallas_call x1, Pallas kernels, step(): pl.pallas_call(step_kernel, out_shape=(jax.ShapeDtypeStruct((16, IMG), f3...  99.6 us
    unnamed x3, local copies, waits for them, and re-layouts  4.91 us

profile of v2, /device:TPU:1, one launch (start us, length us, event | category | flops | bytes accessed | tf_op | source)
XLA Modules:
  0.0 105.1 jit_solution(15930808757999341394)
XLA Ops:
  0.6 99.6 %shard_map.220 = (f32[16,4096]{1,0:T(8,128)}, f32[4,8,2048]{2,1,0:T(8,128)}, f32[32,4,2,32]{3,2,1,0:T(2,128)}) custom-call(bf16[32,256,128]{2,1,0:T(8,128)(2,1)} %bitcast.8, f32[4,8,2048]{2,1,0:T(8,128)} %refs_1_.1, f32[16,4096]{1,0:T(8,128)} %refs_2_.1, bf16[512,256]{1,0:T(8,128)(2,1)} %constant.32.clone.refs_3_, bf16[512,256]{1,0:T(8,128)(2,1)} %constant.33.clone.refs_4_, ...), custom_call_target="tpu_custom_call" | custom-call | tf_op jit(solution)/shard_map/pallas_call | solution.py:638
  100.2 1.7 %copy.27 = f32[16,4096]{1,0:T(8,128)} copy(f32[16,4096]{1,0:T(8,128)} %get-tuple-element.12) | data formatting | bytes 524288
  101.9 1.7 %copy.28 = f32[4,8,2048]{2,1,0:T(8,128)} copy(f32[4,8,2048]{2,1,0:T(8,128)} %get-tuple-element.13) | data formatting | bytes 524288
  103.5 1.6 %copy.29 = f32[1,1,32,4,2,32]{5,4,3,2,1,0:T(2,128)} copy(f32[1,1,32,4,2,32]{5,4,3,2,1,0:T(2,128)} %bitcast.11) | data formatting | bytes 65536

commit v3 on v2

--- a/solution.py
+++ b/solution.py
@@ -501,11 +501,13 @@
     for n in range(16):
         cols = slice(128 * n, 128 * n + 128)
         block = found[16 * n : 16 * n + 16]
-        coeffs[0, :, cols] = block[0:8, :128]
-        coeffs[1, :, cols] = block[0:8, 128:]
-        coeffs[2, :, cols] = block[8:16, :128]
-        coeffs[3, :, cols] = block[8:16, 128:]
+        coeffs[0, :, cols] = coef[0, :, cols] + block[0:8, :128]
+        coeffs[1, :, cols] = coef[1, :, cols] + block[0:8, 128:]
+        coeffs[2, :, cols] = coef[2, :, cols] + block[8:16, :128]
+        coeffs[3, :, cols] = coef[3, :, cols] + block[8:16, 128:]
     abs_total = jnp.sum(jnp.abs(found))
+    out_coeffs = pltpu.make_async_copy(coeffs, r["coeffs"], r["sem_out"].at[1])
+    out_coeffs.start()
 
     def through(rows, cols, spread):
         if spread.dtype == f32:
@@ -556,6 +558,7 @@
     predicted = products.reshape(256, 128)[:, 0:32]
     residual = live * (vis_state + predicted - vis_data)
     resid_square = jnp.sum(residual * residual)
+    r["residual"][...] = residual.reshape(NV, 4, 2, 32)
 
     sent_t, sent_u = r["sent_t"], r["sent_u"]
     spot = lax.broadcasted_iota(jnp.int32, (1, 128), 1)
@@ -566,19 +569,7 @@
     sent_u[...] = jnp.sum(arrived(r, "t", 0, NV)[...], axis=0)
     launch(r, "u", 0, "band", NB, band_me, same=True)
     totals = jnp.sum(arrived(r, "u", 0, NB)[...], axis=0)
-    abs_total, resid_square, data_square = (
-        jnp.sum(jnp.where(spot == n, totals, 0.0), axis=1, keepdims=True) for n in range(3)
-    )
-    threshold = 0.5 * abs_total / (IMG * IMG)
-    for part in range(4):
-        limit = jnp.broadcast_to(threshold, (8, 2048))
-        coeffs[part] = jnp.maximum(jnp.minimum(coef[part] + coeffs[part], limit), -limit)
-    out_coeffs = pltpu.make_async_copy(coeffs, r["coeffs"], r["sem_out"].at[1])
-    out_coeffs.start()
-    radius = 0.5 * jnp.sqrt(data_square + 1e-06)
-    size = jnp.sqrt(resid_square + 1e-06)
-    factor = jnp.broadcast_to(1.0 - jnp.minimum(1.0, radius / size), (256, 32))
-    r["vis_new"][...] = (residual * factor).reshape(NV, 4, 2, 32)
+    r["totals"][...] = totals
 
     for copy in (coef_copy, image_copy):
         copy.wait_send()
@@ -594,7 +585,7 @@
     "vis_state", "vis_data", "rows", "counts", "repeat", "lane_hi", "lane_lo",
     "twist_row", "twists", "order", "sides_hi", "sides_lo",
 ]
-OUTPUTS = ["image", "coeffs", "vis_new"]
+OUTPUTS = ["image", "coeffs", "residual", "totals"]
 VIS_TILE = (2, NV, 2, 8, 128)
 BAND_TILE = (2, NB, 2, 8, 512)
 SCRATCH = dict(
@@ -641,14 +632,60 @@
             jax.ShapeDtypeStruct((16, IMG), f32),
             jax.ShapeDtypeStruct((4, 8, 2048), f32),
             jax.ShapeDtypeStruct((NV, 4, 2, 32), f32),
+            jax.ShapeDtypeStruct((1, 128), f32),
         ),
         in_specs=[anywhere if name in STAGED else vmem for name in INPUTS],
-        out_specs=(anywhere, anywhere, vmem),
+        out_specs=(anywhere, anywhere, vmem, vmem),
         scratch_shapes=scratch,
         compiler_params=pltpu.CompilerParams(
             collective_id=0, has_side_effects=True, vmem_limit_bytes=56 * 2**20
         ),
     )(*[inputs[name] for name in INPUTS])
+
+
+def closing_kernel(*refs):
+    given, out, here, sems = refs[0:4], refs[4:7], refs[7:11], refs[11]
+    copies = [pltpu.make_async_copy(given[n], here[n], sems.at[n]) for n in range(4)]
+    for copy in copies:
+        copy.start()
+
+    def hand_out(n):
+        copies[n] = pltpu.make_async_copy(here[n], out[n], sems.at[n])
+        copies[n].start()
+
+    spot = lax.broadcasted_iota(jnp.int32, (1, 128), 1)
+    copies.pop().wait()
+    copies[0].wait()
+    hand_out(0)
+    abs_total, resid_square, data_square = (
+        jnp.sum(jnp.where(spot == n, here[3][...], 0.0), axis=1, keepdims=True)
+        for n in range(3)
+    )
+    limit = jnp.broadcast_to(0.5 * abs_total / (IMG * IMG), (8, 2048))
+    copies[1].wait()
+    for part in range(4):
+        here[1][part] = jnp.maximum(jnp.minimum(here[1][part], limit), -limit)
+    hand_out(1)
+    radius = 0.5 * jnp.sqrt(data_square + 1e-06)
+    size = jnp.sqrt(resid_square + 1e-06)
+    factor = 1.0 - jnp.minimum(1.0, radius / size)
+    copies[2].wait()
+    here[2][...] = here[2][...] * jnp.broadcast_to(factor.reshape(1, 1, 1, 1), (NV, 4, 2, 32))
+    hand_out(2)
+    for copy in copies:
+        copy.wait()
+
+
+def closing(results):
+    anywhere = pl.BlockSpec(memory_space=pl.ANY)
+    return pl.pallas_call(
+        closing_kernel,
+        out_shape=tuple(jax.ShapeDtypeStruct(x.shape, x.dtype) for x in results[:3]),
+        in_specs=[anywhere] * 4,
+        out_specs=(anywhere,) * 3,
+        scratch_shapes=[pltpu.VMEM(x.shape, x.dtype) for x in results]
+        + [pltpu.SemaphoreType.DMA((4,))],
+    )(*results)
 
 
 def local(sky_image, coef_dual, vis_dual, visibilities, kernel_blocks, tile_rows, tile_counts):
@@ -670,7 +707,7 @@
         rows=tile_rows.reshape(NV, 4).T,
         counts=tile_counts.reshape(1, NV),
     )
-    image, coeffs, vis_new = step(inputs)
+    image, coeffs, vis_new = closing(step(inputs))
     return (image, coeffs, vis_new.reshape(1, 1, NV, 4, 2, 32))
 
 

time: 105 us -> 101 us (0.962)
  local copies, waits for them, and re-layouts: 4.91 us -> 0 us
  Pallas kernels: 99.6 us -> 101 us
    unnamed x3 -> x0, local copies, waits for them, and re-layouts: 4.91 us -> none
    pallas_call x0 -> x1, Pallas kernels: none -> 1.83 us  [closing(): pl.pallas_call(closing_kernel, out_shape=tuple((jax.ShapeDtypeStruct(x.sh...]
where the time goes in v3:
time: 101 us
  Pallas kernels  101 us (100%)
    pallas_call x1, Pallas kernels, step(): pl.pallas_call(step_kernel, out_shape=(jax.ShapeDtypeStruct((16, IMG), f3...  98.8 us

profile of v3, /device:TPU:1, one launch (start us, length us, event | category | flops | bytes accessed | tf_op | source)
XLA Modules:
  0.0 101.3 jit_solution(7692657905170305862)
XLA Ops:
  0.6 98.8 %shard_map.220 = (f32[16,4096]{1,0:T(8,128)}, f32[4,8,2048]{2,1,0:T(8,128)}, f32[32,4,2,32]{3,2,1,0:T(2,128)}, f32[1,128]{1,0:T(1,128)}) custom-call(bf16[32,256,128]{2,1,0:T(8,128)(2,1)} %bitcast.8, f32[4,8,2048]{2,1,0:T(8,128)} %refs_1_.1, f32[16,4096]{1,0:T(8,128)} %refs_2_.1, bf16[512,256]{1,0:T(8,128)(2,1)} %constant.32.clone.refs_3_, ...), custom_call_target="tpu_custom_call" | custom-call | tf_op jit(solution)/shard_map/pallas_call | solution.py:629
  99.4 1.8 %shard_map.221 = (f32[16,4096]{1,0:T(8,128)}, f32[4,8,2048]{2,1,0:T(8,128)}, f32[32,4,2,32]{3,2,1,0:T(2,128)}) custom-call(f32[16,4096]{1,0:T(8,128)} %get-tuple-element.10.refs_0_, f32[4,8,2048]{2,1,0:T(8,128)} %get-tuple-element.11.refs_1_, f32[32,4,2,32]{3,2,1,0:T(2,128)} %get-tuple-element.12.refs_2_, f32[1,128]{1,0:T(1,128)} %get-tuple-element.13.refs_3_), custom_call_target="tpu_custom_call" | custom-call | tf_op jit(solution)/shard_map/pallas_call | solution.py:681

commit v4 on v3

--- a/solution.py
+++ b/solution.py
@@ -199,13 +199,21 @@
     return barrier
 
 
+def far_first(n, count):
+    if count == NV:
+        z, y = n // 8, n // 2 % 4
+        return n % 2 + 2 * (z ^ z // 2) + 8 * (y ^ y // 2)
+    x = n % 4
+    return (x ^ x // 2) + n // 4 * 4
+
+
 def launch(r, name, part, axis, count, me, same=False):
     sent, landed, sems = r["sent_" + name], r["got_" + name].at[part], r["sem_" + name]
     if not same:
         sent = sent.at[part]
 
-    def body(d, carry):
-        peer = me ^ d
+    def body(step, carry):
+        peer = me ^ far_first(count - step, count)
         pltpu.make_async_remote_copy(
             src_ref=sent if same else sent.at[peer],
             dst_ref=landed.at[me],
@@ -271,15 +279,27 @@
     ).astype(f32).astype(bf16)
     column = r["rows"][...]
     facts = jnp.concatenate(
-        [column % 32 * 16 + column // 32 - 256, r["counts"][...], jnp.zeros((3, 32), jnp.int32)],
+        [
+            (column % 32 * 16 + column // 32 - 256).astype(f32),
+            r["counts"][...].astype(f32),
+            jnp.zeros((123, 32), f32),
+        ],
         axis=0,
+    ).astype(bf16)
+    eye = (
+        lax.broadcasted_iota(jnp.int32, (32, 32), 0)
+        == lax.broadcasted_iota(jnp.int32, (32, 32), 1)
     ).astype(f32).astype(bf16)
-    facts = dot_nt(to_row, facts)
-    slot_here = lax.broadcasted_iota(jnp.int32, (256, 8), 0) % 8 // 2
-    fact = lax.broadcasted_iota(jnp.int32, (256, 8), 1)
-    place = jnp.sum(jnp.where(fact == slot_here, facts, 0.0), axis=1, keepdims=True)
-    count = jnp.sum(jnp.where(fact == 4, facts, 0.0), axis=1, keepdims=True)
-    places = jnp.broadcast_to(place, (256, 128)).reshape(NV, 8, 128)
+    facts = dot_nt(eye, facts)
+    r["sent_i"][0] = facts.reshape(NV, 1, 128)
+    row_slot = lax.broadcasted_iota(jnp.int32, (256, 128), 0) % 8 // 2
+    fact = lax.broadcasted_iota(jnp.int32, (256, 128), 1)
+
+    def per_row(table, choice):
+        wide = dot(to_row, table.astype(bf16))
+        return jnp.sum(jnp.where(fact == choice, wide, 0.0), axis=1, keepdims=True)
+
+    count = per_row(facts, 4)
     live = jnp.broadcast_to(count, (256, 32)) > (
         lax.broadcasted_iota(jnp.int32, (256, 32), 0) % 8 // 2
     ).astype(f32)
@@ -306,18 +326,84 @@
         one = jnp.sum(jnp.where(eye, one, 0.0), axis=1, keepdims=True)
         twist_col[:, c] = jnp.broadcast_to(one, (128, 128)).reshape(8, 16, 128)
 
-    sent_a = r["sent_a"].at[0]
+    kernels = staged("kernels")
+    for q in range(NV):
+        r["sent_a"][0, q] = dot(r["weights"][q], kernels[q]).astype(bf16)
     coef = staged("coef")
     for part in range(4):
         r["coef_rows"][3 * part : 3 * part + 3] = coef[part, 5:8, :]
     r["coef_rows"][12:16] = jnp.zeros((4, 2048), f32)
-    kernels = staged("kernels")
-    for q in range(NV):
-        part = dot(r["weights"][q], kernels[q])
-        sent_a[q] = jnp.concatenate([part, places[q]], axis=0).astype(bf16)
     pl.semaphore_wait(barrier, NV + NB)
+    launch(r, "i", 0, "vis", NV, vis_me)
     launch(r, "a", 0, "vis", NV, vis_me)
+
+    order, onehot = r["order"], r["onehot"]
+    where_to = per_row(arrived(r, "i", 0, NV)[...].reshape(NV, 128), row_slot)
+    where_to = jnp.broadcast_to(where_to, (256, 128))
+    lane = lax.broadcasted_iota(jnp.int32, (256, 128), 1).astype(f32)
+    is_imag = lax.broadcasted_iota(jnp.int32, (256, 128), 0) % 2 == 1
+    hots = [(where_to == lane + float(128 * g - 256)).astype(f32) for g in range(4)]
+    for g in range(4):
+        onehot[:, 128 * g : 128 * g + 128] = hots[g].astype(bf16)
+    real_hots = [jnp.where(is_imag, 0.0, h).astype(bf16) for h in hots]
+    imag_hots = [jnp.where(is_imag, h, 0.0).astype(bf16) for h in hots]
+    hots = jnp.concatenate(real_hots + imag_hots, axis=1)
+    contrib = arrived(r, "a", 0, NV)[...].astype(f32).reshape(256, 128).astype(bf16)
+    turned = dot_nt(order[...], contrib).astype(bf16)
+    for part in range(2):
+        grid = dot(turned[64 * part : 64 * part + 64], hots)
+        for c in range(2):
+            for g in range(4):
+                cols = slice(512 * c + 128 * g, 512 * c + 128 * g + 128)
+                for low in range(8):
+                    r["sent_b"][part, low * 4 + g, c] = grid[
+                        8 * low : 8 * low + 8, cols
+                    ].astype(bf16)
+        launch(r, "b", part, "vis", NV, vis_me)
+
+    table_hi, table_lo = staged("table_hi"), staged("table_lo")
+
+    def spread_of(landed):
+        return jnp.concatenate(
+            [landed[:, 0].reshape(256, 128), landed[:, 1].reshape(256, 128)], axis=1
+        )
+
+    first = spread_of(arrived(r, "b", 0, NV))
+    ahead = dot(table_hi[:, 0:256], first) + dot(table_lo[:, 0:256], first)
+    second = spread_of(arrived(r, "b", 1, NV))
+    for part in range(2):
+        both = []
+        for side in range(2):
+            rows = slice(512 * side + 256 * part, 512 * side + 256 * part + 256)
+            both.append(
+                ahead[rows] + dot(table_hi[rows, 256:512], second)
+                + dot(table_lo[rows, 256:512], second)
+            )
+        re = both[0][:, :128] - both[1][:, 128:]
+        im = both[1][:, :128] + both[0][:, 128:]
+        r["sent_c"][part, :, 0] = re.reshape(NV, 8, 128).astype(bf16)
+        r["sent_c"][part, :, 1] = im.reshape(NV, 8, 128).astype(bf16)
+        launch(r, "c", part, "vis", NV, vis_me)
     coef_copy = to_neighbour(r["coef_rows"], r["got_coef"], r["sem_coef"], following)
+
+    sent_d = r["sent_d"]
+    for part in range(2):
+        got_c = arrived(r, "c", part, NV)
+        rows = slice(8 * part, 8 * part + 8)
+        for g in range(4):
+            values = []
+            for low in range(8):
+                re = got_c[low * 4 + g, 0].astype(f32)
+                im = got_c[low * 4 + g, 1].astype(f32)
+                cosine, sine = twist_col[low, 0, rows], twist_col[low, 1, rows]
+                values.append((re * cosine - im * sine, re * sine + im * cosine))
+            values = small_dft(values, 1.0)
+            for b in range(NB):
+                for c in range(2):
+                    sent_d[part, b, c, :, 128 * g : 128 * g + 128] = values[b][c].astype(
+                        sent_d.dtype
+                    )
+        launch(r, "d", part, "band", NB, band_me)
 
     sky = staged("sky")
     sides_hi, sides_lo = r["sides_hi"], r["sides_lo"]
@@ -340,73 +426,6 @@
     for n in range(16):
         cols = slice(256 * n, 256 * n + 256)
         raw[:, cols] = sky[:, cols] - smooth[16 * n : 16 * n + 16]
-    got_a = arrived(r, "a", 0, NV)
-
-    order, onehot = r["order"], r["onehot"]
-    contrib = got_a[:, 0:8, :].astype(f32).reshape(256, 128).astype(bf16)
-    where_to = got_a[:, 8:16, :].astype(f32).reshape(256, 128)
-    lane = lax.broadcasted_iota(jnp.int32, (256, 128), 1).astype(f32)
-    is_imag = lax.broadcasted_iota(jnp.int32, (256, 128), 0) % 2 == 1
-    hots = [(where_to == lane + float(128 * g - 256)).astype(f32) for g in range(4)]
-    for g in range(4):
-        onehot[:, 128 * g : 128 * g + 128] = hots[g].astype(bf16)
-    real_hots = [jnp.where(is_imag, 0.0, h).astype(bf16) for h in hots]
-    imag_hots = [jnp.where(is_imag, h, 0.0).astype(bf16) for h in hots]
-    hots = jnp.concatenate(real_hots + imag_hots, axis=1)
-    turned = dot_nt(order[...], contrib).astype(bf16)
-    for part in range(2):
-        grid = dot(turned[64 * part : 64 * part + 64], hots)
-        for c in range(2):
-            for g in range(4):
-                cols = slice(512 * c + 128 * g, 512 * c + 128 * g + 128)
-                for low in range(8):
-                    r["sent_b"][part, low * 4 + g, c] = grid[
-                        8 * low : 8 * low + 8, cols
-                    ].astype(bf16)
-        launch(r, "b", part, "vis", NV, vis_me)
-
-    table_hi, table_lo = staged("table_hi"), staged("table_lo")
-
-    def spread_of(landed):
-        return jnp.concatenate(
-            [landed[:, 0].reshape(256, 128), landed[:, 1].reshape(256, 128)], axis=1
-        )
-
-    first = spread_of(arrived(r, "b", 0, NV))
-    ahead = dot(table_hi[:, 0:256], first) + dot(table_lo[:, 0:256], first)
-    second = spread_of(arrived(r, "b", 1, NV))
-    for part in range(2):
-        both = []
-        for side in range(2):
-            rows = slice(512 * side + 256 * part, 512 * side + 256 * part + 256)
-            both.append(
-                ahead[rows] + dot(table_hi[rows, 256:512], second)
-                + dot(table_lo[rows, 256:512], second)
-            )
-        re = both[0][:, :128] - both[1][:, 128:]
-        im = both[1][:, :128] + both[0][:, 128:]
-        r["sent_c"][part, :, 0] = re.reshape(NV, 8, 128).astype(bf16)
-        r["sent_c"][part, :, 1] = im.reshape(NV, 8, 128).astype(bf16)
-        launch(r, "c", part, "vis", NV, vis_me)
-
-    sent_d = r["sent_d"]
-    for part in range(2):
-        got_c = arrived(r, "c", part, NV)
-        rows = slice(8 * part, 8 * part + 8)
-        for g in range(4):
-            values = []
-            for low in range(8):
-                re = got_c[low * 4 + g, 0].astype(f32)
-                im = got_c[low * 4 + g, 1].astype(f32)
-                cosine, sine = twist_col[low, 0, rows], twist_col[low, 1, rows]
-                values.append((re * cosine - im * sine, re * sine + im * cosine))
-            values = small_dft(values, 1.0)
-            for b in range(NB):
-                for c in range(2):
-                    sent_d[part, b, c, :, 128 * g : 128 * g + 128] = values[b][c].astype(
-                        sent_d.dtype
-                    )
-        launch(r, "d", part, "band", NB, band_me)
 
     mid, twist_row, extrap, sent_e = r["mid"], r["twist_row"], r["extrap"], r["sent_e"]
 
@@ -575,7 +594,7 @@
         copy.wait_send()
     out_image.wait()
     out_coeffs.wait()
-    for name in "abcdefghtu":
+    for name in "abcdefghitu":
         for part in range(2 if name in "bcdefg" else 1):
             finish(r, name, part, NB if name in "deu" else NV, 0)
 
@@ -598,7 +617,8 @@
     here_table_lo=((1024, 512), bf16),
     here_down_hi=((384, 256), bf16),
     here_down_lo=((384, 256), bf16),
-    sent_a=((1, NV, 16, 128), bf16), got_a=((1, NV, 16, 128), bf16),
+    sent_a=((1, NV, 8, 128), bf16), got_a=((1, NV, 8, 128), bf16),
+    sent_i=((1, NV, 1, 128), f32), got_i=((1, NV, 1, 128), f32),
     sent_b=(VIS_TILE, bf16), got_b=(VIS_TILE, bf16),
     sent_c=(VIS_TILE, bf16), got_c=(VIS_TILE, bf16),
     sent_d=(BAND_TILE, bf16), got_d=(BAND_TILE, bf16),
@@ -612,7 +632,7 @@
     got_coef=((16, 2048), f32), got_rows=((8, IMG), f32),
     raw_here=((16, IMG), f32), extrap=((2, 8, IMG), f32), coeffs_here=((4, 8, 2048), f32),
     onehot=((256, 512), bf16), mid=((2, 32, 2, 8, 128), f32),
-    **{"sem_" + n: 4 for n in list("abcdefghtu") + ["coef", "rows", "out"]},
+    **{"sem_" + n: 4 for n in list("abcdefghitu") + ["coef", "rows", "out"]},
     sem_in=len(STAGED),
 )
 

time: 101 us -> 96 us (0.950)
  Pallas kernels: 101 us -> 95.3 us
    pallas_call x1, Pallas kernels: 98.8 us -> 93.4 us  [step(): pl.pallas_call(step_kernel, out_shape=(jax.ShapeDtypeStruct((16, IMG), f3...]
where the time goes in v4:
time: 96 us; the launch traced here: 95.9 us
  Pallas kernels  95.3 us (99%)
    pallas_call x1, Pallas kernels, step(): pl.pallas_call(step_kernel, out_shape=(jax.ShapeDtypeStruct((16, IMG), f3...  93.4 us

profile of v4, /device:TPU:1, one launch (start us, length us, event | category | flops | bytes accessed | tf_op | source)
XLA Modules:
  0.0 95.9 jit_solution(4815036740270000670)
XLA Ops:
  0.6 93.4 %shard_map.220 = (f32[16,4096]{1,0:T(8,128)}, f32[4,8,2048]{2,1,0:T(8,128)}, f32[32,4,2,32]{3,2,1,0:T(2,128)}, f32[1,128]{1,0:T(1,128)}) custom-call(bf16[32,256,128]{2,1,0:T(8,128)(2,1)} %bitcast.8, f32[4,8,2048]{2,1,0:T(8,128)} %refs_1_.1, f32[16,4096]{1,0:T(8,128)} %refs_2_.1, bf16[512,256]{1,0:T(8,128)(2,1)} %constant.32.clone.refs_3_, ...), custom_call_target="tpu_custom_call" | custom-call | tf_op jit(solution)/shard_map/pallas_call | solution.py:649
  94.1 1.8 %shard_map.221 = (f32[16,4096]{1,0:T(8,128)}, f32[4,8,2048]{2,1,0:T(8,128)}, f32[32,4,2,32]{3,2,1,0:T(2,128)}) custom-call(f32[16,4096]{1,0:T(8,128)} %get-tuple-element.10.refs_0_, f32[4,8,2048]{2,1,0:T(8,128)} %get-tuple-element.11.refs_1_, f32[32,4,2,32]{3,2,1,0:T(2,128)} %get-tuple-element.12.refs_2_, f32[1,128]{1,0:T(1,128)} %get-tuple-element.13.refs_3_), custom_call_target="tpu_custom_call" | custom-call | tf_op jit(solution)/shard_map/pallas_call | solution.py:701

commit v5 on v4

--- a/solution.py
+++ b/solution.py
@@ -177,6 +177,10 @@
     return dot(high, value_high) + dot(high, value_low) + dot(low, value_high)
 
 
+def dropped(value):
+    return value - value.astype(bf16).astype(f32)
+
+
 def greet(vis_me, band_me, neighbours):
     barrier = pltpu.get_barrier_semaphore()
 
@@ -226,6 +230,43 @@
 
     lax.fori_loop(1, count, body, 0)
     landed[me] = sent[...] if same else sent[me]
+
+
+def rest_copy(r, part, low, me):
+    return pltpu.make_async_remote_copy(
+        src_ref=r["sent_l"].at[part, low],
+        dst_ref=r["got_l"].at[part, me],
+        send_sem=r["sem_l"].at[2 * part],
+        recv_sem=r["sem_l"].at[2 * part + 1],
+        device_id={"vis": 4 * low},
+        device_id_type=MESH_ID,
+    )
+
+
+def launch_rest(r, part, me):
+    for low in range(8):
+
+        @pl.when(me != 4 * low)
+        def _():
+            rest_copy(r, part, low, me).start()
+
+        @pl.when(me == 4 * low)
+        def _():
+            r["got_l"][part, me] = r["sent_l"][part, low]
+
+
+def rest_arrived(r, part, me):
+    @pl.when(me % 4 == 0)
+    def _():
+        finish(r, "l", part, NV, 1)
+
+
+def rest_drained(r, part, me):
+    finish(r, "l", part, 8, 0)
+
+    @pl.when(me % 4 != 0)
+    def _():
+        finish(r, "l", part, 2, 0)
 
 
 def to_neighbour(sent, landed, sems, neighbour):
@@ -333,6 +374,7 @@
     for part in range(4):
         r["coef_rows"][3 * part : 3 * part + 3] = coef[part, 5:8, :]
     r["coef_rows"][12:16] = jnp.zeros((4, 2048), f32)
+    r["got_l"][...] = jnp.zeros((2, NV, 8, 128), bf16)
     pl.semaphore_wait(barrier, NV + NB)
     launch(r, "i", 0, "vis", NV, vis_me)
     launch(r, "a", 0, "vis", NV, vis_me)
@@ -428,6 +470,9 @@
         raw[:, cols] = sky[:, cols] - smooth[16 * n : 16 * n + 16]
 
     mid, twist_row, extrap, sent_e = r["mid"], r["twist_row"], r["extrap"], r["sent_e"]
+
+    first_lane = lax.broadcasted_iota(jnp.int32, (8, 128), 1) == 0
+    second_lane = lax.broadcasted_iota(jnp.int32, (8, 128), 1) == 1
 
     def lane_product(part):
         return by_table(
@@ -472,38 +517,49 @@
                 mid[part, a, 1] = im * cosine - re * sine
         lanes = lane_product(part)
         for g in range(4):
-            for c in range(2):
-                parts = []
-                for a in range(8):
-                    re, im = lanes[g * 8 + a, 0], lanes[g * 8 + a, 1]
-                    if c == 0:
-                        parts.append(re[:, :128] + im[:, 128:])
-                    else:
-                        parts.append(im[:, :128] - re[:, 128:])
-                parts = swap_groups(parts)
-                for b in range(NB):
-                    sent_e[part, b, c, :, 128 * g : 128 * g + 128] = parts[b]
+            cols = slice(128 * g, 128 * g + 128)
+            reals, imags = [], []
+            for a in range(8):
+                re, im = lanes[g * 8 + a, 0], lanes[g * 8 + a, 1]
+                reals.append(re[:, :128] + im[:, 128:])
+                imags.append(im[:, :128] - re[:, 128:])
+            reals, imags = swap_groups(reals), swap_groups(imags)
+            if g == 0:
+                imags[0] = jnp.where(first_lane, dropped(reals[0]), imags[0])
+            for b in range(NB):
+                sent_e[part, b, 0, :, cols] = reals[b].astype(bf16)
+                sent_e[part, b, 1, :, cols] = imags[b].astype(bf16)
         launch(r, "e", part, "band", NB, band_me)
     out_image = pltpu.make_async_copy(raw, r["image"], r["sem_out"].at[0])
     out_image.start()
 
     sent_f = r["sent_f"]
+    column_zero = jnp.where(first_lane, jnp.where(band_me == 0, 1.0, 0.0), 0.0)
     for part in range(2):
         got_e = arrived(r, "e", part, NB)
         rows = slice(8 * part, 8 * part + 8)
         for g in range(4):
             values = []
             for b in range(NB):
-                values.append(
-                    tuple(got_e[b, c, :, 128 * g : 128 * g + 128] for c in range(2))
+                re, im = (
+                    got_e[b, c, :, 128 * g : 128 * g + 128].astype(f32) for c in range(2)
                 )
+                if g == 0:
+                    re, im = re + im * column_zero, im * (1.0 - column_zero)
+                values.append((re, im))
             values = small_dft(values, -1.0)
             for low in range(8):
                 re, im = values[low]
                 cosine, sine = twist_col[low, 0, rows], twist_col[low, 1, rows]
-                sent_f[part, low * 4 + g, 0] = (re * cosine + im * sine).astype(sent_f.dtype)
-                sent_f[part, low * 4 + g, 1] = (im * cosine - re * sine).astype(sent_f.dtype)
+                re, im = re * cosine + im * sine, im * cosine - re * sine
+                sent_f[part, low * 4 + g, 0] = re.astype(bf16)
+                sent_f[part, low * 4 + g, 1] = im.astype(bf16)
+                if g == 0:
+                    rest = jnp.where(first_lane, dropped(re), 0.0)
+                    rest = jnp.where(second_lane, pltpu.roll(dropped(im), 1, 1), rest)
+                    r["sent_l"][part, low] = rest.astype(bf16)
         launch(r, "f", part, "vis", NV, vis_me)
+        launch_rest(r, part, vis_me)
 
     down_hi, down_lo = staged("down_hi"), staged("down_lo")
     image_copy.wait_recv()
@@ -528,19 +584,27 @@
     out_coeffs = pltpu.make_async_copy(coeffs, r["coeffs"], r["sem_out"].at[1])
     out_coeffs.start()
 
-    def through(rows, cols, spread):
-        if spread.dtype == f32:
-            return table_by(table_hi[rows, cols], table_lo[rows, cols], spread)
-        return dot(table_hi[rows, cols], spread) + dot(table_lo[rows, cols], spread)
+    def through(rows, cols, spread, rest):
+        wide = dot(table_hi[rows, cols], spread) + dot(table_lo[rows, cols], spread)
+        rest = dot(table_hi[rows, cols], rest)
+        one = lax.broadcasted_iota(jnp.int32, rest.shape, 1) == 0
+        return wide + jnp.concatenate(
+            [jnp.where(one, rest, 0.0), jnp.where(one, pltpu.roll(rest, 127, 1), 0.0)], axis=1
+        )
+
+    def rest_of(part):
+        rest_arrived(r, part, vis_me)
+        return r["got_l"][part].astype(f32).reshape(256, 128).astype(bf16)
 
     first = spread_of(arrived(r, "f", 0, NV))
-    ahead = through(slice(0, 1024), slice(0, 256), first)
+    ahead = through(slice(0, 1024), slice(0, 256), first, rest_of(0))
     second = spread_of(arrived(r, "f", 1, NV))
+    rest = rest_of(1)
     for part in range(2):
         both = []
         for side in range(2):
             rows = slice(512 * side + 256 * part, 512 * side + 256 * part + 256)
-            both.append(ahead[rows] + through(rows, slice(256, 512), second))
+            both.append(ahead[rows] + through(rows, slice(256, 512), second, rest))
         re = both[0][:, :128] + both[1][:, 128:]
         im = both[0][:, 128:] - both[1][:, :128]
         r["sent_g"][part, :, 0] = re.reshape(NV, 8, 128).astype(bf16)
@@ -597,6 +661,8 @@
     for name in "abcdefghitu":
         for part in range(2 if name in "bcdefg" else 1):
             finish(r, name, part, NB if name in "deu" else NV, 0)
+    for part in range(2):
+        rest_drained(r, part, vis_me)
 
 
 STAGED = ["kernels", "coef", "sky", "up_hi", "up_lo", "table_hi", "table_lo", "down_hi", "down_lo"]
@@ -622,8 +688,9 @@
     sent_b=(VIS_TILE, bf16), got_b=(VIS_TILE, bf16),
     sent_c=(VIS_TILE, bf16), got_c=(VIS_TILE, bf16),
     sent_d=(BAND_TILE, bf16), got_d=(BAND_TILE, bf16),
-    sent_e=(BAND_TILE, f32), got_e=(BAND_TILE, f32),
-    sent_f=(VIS_TILE, f32), got_f=(VIS_TILE, f32),
+    sent_e=(BAND_TILE, bf16), got_e=(BAND_TILE, bf16),
+    sent_f=(VIS_TILE, bf16), got_f=(VIS_TILE, bf16),
+    sent_l=((2, 8, 8, 128), bf16), got_l=((2, NV, 8, 128), bf16),
     sent_g=(VIS_TILE, bf16), got_g=(VIS_TILE, bf16),
     sent_h=((1, NV, 8, 128), bf16), got_h=((1, NV, 8, 128), bf16),
     sent_t=((1, 128), f32), got_t=((1, NV, 1, 128), f32),
@@ -632,7 +699,7 @@
     got_coef=((16, 2048), f32), got_rows=((8, IMG), f32),
     raw_here=((16, IMG), f32), extrap=((2, 8, IMG), f32), coeffs_here=((4, 8, 2048), f32),
     onehot=((256, 512), bf16), mid=((2, 32, 2, 8, 128), f32),
-    **{"sem_" + n: 4 for n in list("abcdefghitu") + ["coef", "rows", "out"]},
+    **{"sem_" + n: 4 for n in list("abcdefghiltu") + ["coef", "rows", "out"]},
     sem_in=len(STAGED),
 )
 

time: 96 us -> 89.2 us (0.929)
  Pallas kernels: 95.3 us -> 88.5 us
    pallas_call x1, Pallas kernels: 93.4 us -> 86.6 us  [step(): pl.pallas_call(step_kernel, out_shape=(jax.ShapeDtypeStruct((16, IMG), f3...]
where the time goes in v5:
time: 89.2 us; the launch traced here: 89.1 us
  Pallas kernels  88.5 us (99%)
    pallas_call x1, Pallas kernels, step(): pl.pallas_call(step_kernel, out_shape=(jax.ShapeDtypeStruct((16, IMG), f3...  86.6 us
    pallas_call x1, Pallas kernels, closing(): pl.pallas_call(closing_kernel, out_shape=tuple((jax.ShapeDtypeStruct(x.sh...  1.83 us

profile of v5, /device:TPU:1, one launch (start us, length us, event | category | flops | bytes accessed | tf_op | source)
XLA Modules:
  0.0 89.1 jit_solution(10136617366136911703)
XLA Ops:
  0.6 86.6 %shard_map.220 = (f32[16,4096]{1,0:T(8,128)}, f32[4,8,2048]{2,1,0:T(8,128)}, f32[32,4,2,32]{3,2,1,0:T(2,128)}, f32[1,128]{1,0:T(1,128)}) custom-call(bf16[32,256,128]{2,1,0:T(8,128)(2,1)} %bitcast.8, f32[4,8,2048]{2,1,0:T(8,128)} %refs_1_.1, f32[16,4096]{1,0:T(8,128)} %refs_2_.1, bf16[512,256]{1,0:T(8,128)(2,1)} %constant.32.clone.refs_3_, ...), custom_call_target="tpu_custom_call" | custom-call | tf_op jit(solution)/shard_map/pallas_call | solution.py:716
  87.3 1.8 %shard_map.221 = (f32[16,4096]{1,0:T(8,128)}, f32[4,8,2048]{2,1,0:T(8,128)}, f32[32,4,2,32]{3,2,1,0:T(2,128)}) custom-call(f32[16,4096]{1,0:T(8,128)} %get-tuple-element.10.refs_0_, f32[4,8,2048]{2,1,0:T(8,128)} %get-tuple-element.11.refs_1_, f32[32,4,2,32]{3,2,1,0:T(2,128)} %get-tuple-element.12.refs_2_, f32[1,128]{1,0:T(1,128)} %get-tuple-element.13.refs_3_), custom_call_target="tpu_custom_call" | custom-call | tf_op jit(solution)/shard_map/pallas_call | solution.py:768

commit v6 on v5

--- a/solution.py
+++ b/solution.py
@@ -137,20 +137,22 @@
     return out
 
 
-def swap_groups(arrays):
+def swap_groups(arrays, width=16):
     arrays = list(arrays)
-    lane = lax.broadcasted_iota(jnp.int32, arrays[0].shape, arrays[0].ndim - 1)
     axis = arrays[0].ndim - 1
-    for bit in range(3):
-        shift = 16 << bit
+    lane = lax.broadcasted_iota(jnp.int32, arrays[0].shape, axis)
+    bit = 1
+    while bit < len(arrays):
+        shift = width * bit
         upper = (lane // shift) % 2 == 1
-        for j in range(8):
-            other = j | (1 << bit)
+        for j in range(len(arrays)):
+            other = j | bit
             if other == j:
                 continue
             low, high = arrays[j], arrays[other]
             arrays[j] = jnp.where(upper, pltpu.roll(high, shift, axis), low)
             arrays[other] = jnp.where(upper, high, pltpu.roll(low, 128 - shift, axis))
+        bit *= 2
     return arrays
 
 
@@ -332,7 +334,12 @@
         == lax.broadcasted_iota(jnp.int32, (32, 32), 1)
     ).astype(f32).astype(bf16)
     facts = dot_nt(eye, facts)
-    r["sent_i"][0] = facts.reshape(NV, 1, 128)
+    place = (column % 32 * 16 + column // 32 - 256).astype(f32)
+    r["sent_i"][...] = jnp.concatenate([place[n : n + 1] for n in range(4)], axis=1)
+    row, col = (lax.broadcasted_iota(jnp.int32, (256, 256), n) for n in range(2))
+    source = row // 8 % 8 * 32 + row % 2 * 16 + row // 64 * 4 + row % 8 // 2
+    r["reorder"][...] = (col == source).astype(f32).astype(bf16)
+    r["blocks"][...] = jnp.zeros((4, 128, 1024), bf16)
     row_slot = lax.broadcasted_iota(jnp.int32, (256, 128), 0) % 8 // 2
     fact = lax.broadcasted_iota(jnp.int32, (256, 128), 1)
 
@@ -376,17 +383,17 @@
     r["coef_rows"][12:16] = jnp.zeros((4, 2048), f32)
     r["got_l"][...] = jnp.zeros((2, NV, 8, 128), bf16)
     pl.semaphore_wait(barrier, NV + NB)
-    launch(r, "i", 0, "vis", NV, vis_me)
+    launch(r, "i", 0, "vis", NV, vis_me, same=True)
     launch(r, "a", 0, "vis", NV, vis_me)
-
-    order, onehot = r["order"], r["onehot"]
-    where_to = per_row(arrived(r, "i", 0, NV)[...].reshape(NV, 128), row_slot)
+    coef_copy = to_neighbour(r["coef_rows"], r["got_coef"], r["sem_coef"], following)
+
+    order = r["order"]
+    positions = arrived(r, "i", 0, NV)[...].reshape(NV, 128)
+    where_to = per_row(positions, 32 * row_slot + vis_me)
     where_to = jnp.broadcast_to(where_to, (256, 128))
     lane = lax.broadcasted_iota(jnp.int32, (256, 128), 1).astype(f32)
     is_imag = lax.broadcasted_iota(jnp.int32, (256, 128), 0) % 2 == 1
     hots = [(where_to == lane + float(128 * g - 256)).astype(f32) for g in range(4)]
-    for g in range(4):
-        onehot[:, 128 * g : 128 * g + 128] = hots[g].astype(bf16)
     real_hots = [jnp.where(is_imag, 0.0, h).astype(bf16) for h in hots]
     imag_hots = [jnp.where(is_imag, h, 0.0).astype(bf16) for h in hots]
     hots = jnp.concatenate(real_hots + imag_hots, axis=1)
@@ -403,49 +410,19 @@
                     ].astype(bf16)
         launch(r, "b", part, "vis", NV, vis_me)
 
-    table_hi, table_lo = staged("table_hi"), staged("table_lo")
-
-    def spread_of(landed):
-        return jnp.concatenate(
-            [landed[:, 0].reshape(256, 128), landed[:, 1].reshape(256, 128)], axis=1
-        )
-
-    first = spread_of(arrived(r, "b", 0, NV))
-    ahead = dot(table_hi[:, 0:256], first) + dot(table_lo[:, 0:256], first)
-    second = spread_of(arrived(r, "b", 1, NV))
-    for part in range(2):
-        both = []
-        for side in range(2):
-            rows = slice(512 * side + 256 * part, 512 * side + 256 * part + 256)
-            both.append(
-                ahead[rows] + dot(table_hi[rows, 256:512], second)
-                + dot(table_lo[rows, 256:512], second)
-            )
-        re = both[0][:, :128] - both[1][:, 128:]
-        im = both[1][:, :128] + both[0][:, 128:]
-        r["sent_c"][part, :, 0] = re.reshape(NV, 8, 128).astype(bf16)
-        r["sent_c"][part, :, 1] = im.reshape(NV, 8, 128).astype(bf16)
-        launch(r, "c", part, "vis", NV, vis_me)
-    coef_copy = to_neighbour(r["coef_rows"], r["got_coef"], r["sem_coef"], following)
-
-    sent_d = r["sent_d"]
-    for part in range(2):
-        got_c = arrived(r, "c", part, NV)
-        rows = slice(8 * part, 8 * part + 8)
-        for g in range(4):
-            values = []
-            for low in range(8):
-                re = got_c[low * 4 + g, 0].astype(f32)
-                im = got_c[low * 4 + g, 1].astype(f32)
-                cosine, sine = twist_col[low, 0, rows], twist_col[low, 1, rows]
-                values.append((re * cosine - im * sine, re * sine + im * cosine))
-            values = small_dft(values, 1.0)
-            for b in range(NB):
-                for c in range(2):
-                    sent_d[part, b, c, :, 128 * g : 128 * g + 128] = values[b][c].astype(
-                        sent_d.dtype
-                    )
-        launch(r, "d", part, "band", NB, band_me)
+    to_row = (
+        lax.broadcasted_iota(jnp.int32, (128, 32), 0) // 4
+        == lax.broadcasted_iota(jnp.int32, (128, 32), 1)
+    ).astype(f32).astype(bf16)
+    row, lane = (lax.broadcasted_iota(jnp.int32, (128, 128), n) for n in range(2))
+    wide = jnp.where(lane // 32 == row % 4, dot(to_row, positions.astype(bf16)), 0.0)
+    wide = wide + pltpu.roll(wide, 64, 1)
+    wide = wide + pltpu.roll(wide, 32, 1)
+    here = (lane + 128 * (vis_me % 4) - 256).astype(f32)
+    for q in range(NV):
+        hot = jnp.broadcast_to(wide[:, q : q + 1], (128, 128)) == here
+        cols = slice(128 * (q % 8), 128 * (q % 8) + 128)
+        r["hots"][q // 8, :, cols] = hot.astype(f32).astype(bf16)
 
     sky = staged("sky")
     sides_hi, sides_lo = r["sides_hi"], r["sides_lo"]
@@ -468,6 +445,49 @@
     for n in range(16):
         cols = slice(256 * n, 256 * n + 256)
         raw[:, cols] = sky[:, cols] - smooth[16 * n : 16 * n + 16]
+
+    table_hi, table_lo = staged("table_hi"), staged("table_lo")
+
+    def spread_of(landed):
+        return jnp.concatenate(
+            [landed[:, 0].reshape(256, 128), landed[:, 1].reshape(256, 128)], axis=1
+        )
+
+    first = spread_of(arrived(r, "b", 0, NV))
+    ahead = dot(table_hi[:, 0:256], first) + dot(table_lo[:, 0:256], first)
+    second = spread_of(arrived(r, "b", 1, NV))
+    for part in range(2):
+        both = []
+        for side in range(2):
+            rows = slice(512 * side + 256 * part, 512 * side + 256 * part + 256)
+            both.append(
+                ahead[rows] + dot(table_hi[rows, 256:512], second)
+                + dot(table_lo[rows, 256:512], second)
+            )
+        re = both[0][:, :128] - both[1][:, 128:]
+        im = both[1][:, :128] + both[0][:, 128:]
+        r["sent_c"][part, :, 0] = re.reshape(NV, 8, 128).astype(bf16)
+        r["sent_c"][part, :, 1] = im.reshape(NV, 8, 128).astype(bf16)
+        launch(r, "c", part, "vis", NV, vis_me)
+
+    sent_d = r["sent_d"]
+    for part in range(2):
+        got_c = arrived(r, "c", part, NV)
+        rows = slice(8 * part, 8 * part + 8)
+        for g in range(4):
+            values = []
+            for low in range(8):
+                re = got_c[low * 4 + g, 0].astype(f32)
+                im = got_c[low * 4 + g, 1].astype(f32)
+                cosine, sine = twist_col[low, 0, rows], twist_col[low, 1, rows]
+                values.append((re * cosine - im * sine, re * sine + im * cosine))
+            values = small_dft(values, 1.0)
+            for b in range(NB):
+                for c in range(2):
+                    sent_d[part, b, c, :, 128 * g : 128 * g + 128] = values[b][c].astype(
+                        sent_d.dtype
+                    )
+        launch(r, "d", part, "band", NB, band_me)
 
     mid, twist_row, extrap, sent_e = r["mid"], r["twist_row"], r["extrap"], r["sent_e"]
 
@@ -502,8 +522,6 @@
             now = jnp.maximum(raw[rows, cols] - values[n][0], 0.0)
             raw[rows, cols] = now
             extrap[part, :, cols] = 2.0 * now - sky[rows, cols]
-        if part == 0:
-            image_copy = to_neighbour(extrap.at[0], r["got_rows"], r["sem_rows"], preceding)
         values = [(extrap[part, :, 128 * n : 128 * n + 128], None) for n in range(32)]
         values = small_dft(values, -1.0)
         for a in range(32):
@@ -560,6 +578,48 @@
                     r["sent_l"][part, low] = rest.astype(bf16)
         launch(r, "f", part, "vis", NV, vis_me)
         launch_rest(r, part, vis_me)
+    image_copy = to_neighbour(extrap.at[0], r["got_rows"], r["sem_rows"], preceding)
+
+    def through(rows, cols, spread, rest):
+        wide = dot(table_hi[rows, cols], spread) + dot(table_lo[rows, cols], spread)
+        rest = dot(table_hi[rows, cols], rest)
+        one = lax.broadcasted_iota(jnp.int32, rest.shape, 1) == 0
+        return wide + jnp.concatenate(
+            [jnp.where(one, rest, 0.0), jnp.where(one, pltpu.roll(rest, 127, 1), 0.0)], axis=1
+        )
+
+    def rest_of(part):
+        rest_arrived(r, part, vis_me)
+        return r["got_l"][part].astype(f32).reshape(256, 128).astype(bf16)
+
+    first = spread_of(arrived(r, "f", 0, NV))
+    ahead = through(slice(0, 1024), slice(0, 256), first, rest_of(0))
+    second = spread_of(arrived(r, "f", 1, NV))
+    rest = rest_of(1)
+    for part in range(2):
+        both = []
+        for side in range(2):
+            rows = slice(512 * side + 256 * part, 512 * side + 256 * part + 256)
+            both.append(ahead[rows] + through(rows, slice(256, 512), second, rest))
+        re = both[0][:, :128] + both[1][:, 128:]
+        im = both[0][:, 128:] - both[1][:, :128]
+        for q in range(NV):
+            rows, cols = (slice(n * (q % 8), n * (q % 8) + n) for n in (16, 128))
+            r["blocks"][q // 8, rows, cols] = jnp.concatenate(
+                [re[8 * q : 8 * q + 8], im[8 * q : 8 * q + 8]], axis=0
+            ).astype(bf16)
+        picked = [
+            dot_nt(r["hots"][n], r["blocks"][n]).reshape(16, 8, 128) for n in range(4)
+        ]
+        upper = lax.broadcasted_iota(jnp.int32, (16, 8, 128), 1) < 4
+        chunks = []
+        for n in (0, 2):
+            one, two = picked[n], picked[n + 1]
+            even = jnp.where(upper, one, pltpu.roll(two, 4, 1))
+            odd = jnp.where(upper, pltpu.roll(one, 4, 1), two)
+            chunks.append(jnp.stack([even, odd], axis=1).reshape(NV, 8, 128))
+        r["sent_g"][part] = jnp.concatenate(chunks, axis=1).astype(bf16)
+        launch(r, "g", part, "vis", NV, vis_me)
 
     down_hi, down_lo = staged("down_hi"), staged("down_lo")
     image_copy.wait_recv()
@@ -583,53 +643,16 @@
     abs_total = jnp.sum(jnp.abs(found))
     out_coeffs = pltpu.make_async_copy(coeffs, r["coeffs"], r["sem_out"].at[1])
     out_coeffs.start()
-
-    def through(rows, cols, spread, rest):
-        wide = dot(table_hi[rows, cols], spread) + dot(table_lo[rows, cols], spread)
-        rest = dot(table_hi[rows, cols], rest)
-        one = lax.broadcasted_iota(jnp.int32, rest.shape, 1) == 0
-        return wide + jnp.concatenate(
-            [jnp.where(one, rest, 0.0), jnp.where(one, pltpu.roll(rest, 127, 1), 0.0)], axis=1
-        )
-
-    def rest_of(part):
-        rest_arrived(r, part, vis_me)
-        return r["got_l"][part].astype(f32).reshape(256, 128).astype(bf16)
-
-    first = spread_of(arrived(r, "f", 0, NV))
-    ahead = through(slice(0, 1024), slice(0, 256), first, rest_of(0))
-    second = spread_of(arrived(r, "f", 1, NV))
-    rest = rest_of(1)
-    for part in range(2):
-        both = []
-        for side in range(2):
-            rows = slice(512 * side + 256 * part, 512 * side + 256 * part + 256)
-            both.append(ahead[rows] + through(rows, slice(256, 512), second, rest))
-        re = both[0][:, :128] + both[1][:, 128:]
-        im = both[0][:, 128:] - both[1][:, :128]
-        r["sent_g"][part, :, 0] = re.reshape(NV, 8, 128).astype(bf16)
-        r["sent_g"][part, :, 1] = im.reshape(NV, 8, 128).astype(bf16)
-        launch(r, "g", part, "vis", NV, vis_me)
-
-    picked = [[], []]
+    values = []
     for part in range(2):
         got_g = arrived(r, "g", part, NV)
-        for c in range(2):
-            total = 0.0
-            for g in range(4):
-                piece = jnp.concatenate(
-                    [got_g[low * 4 + g, c].astype(f32) for low in range(8)], axis=0
-                ).astype(bf16)
-                total = total + dot_nt(onehot[:, 128 * g : 128 * g + 128], piece)
-            picked[c].append(total)
-    picked = [jnp.concatenate(p, axis=1) for p in picked]
-    tiles = jnp.where(is_imag, picked[1], picked[0]).astype(bf16)
-    tiles = dot(tiles, order[...])
-    r["sent_h"][0] = tiles.reshape(NV, 8, 128).astype(bf16)
-    launch(r, "h", 0, "vis", NV, vis_me)
-    got_h = arrived(r, "h", 0, NV)
-
-    products = jnp.stack([dot_nt(got_h[q], kernels[q]) for q in range(NV)])
+        for low in range(8):
+            first, second, third, fourth = (got_g[4 * low + g].astype(f32) for g in range(4))
+            values.append((first + second) + (third + fourth))
+    tiles = jnp.concatenate(swap_groups(values, 8), axis=0).astype(bf16)
+    tiles = dot(r["reorder"][...], tiles).astype(bf16)
+    tiles = dot(tiles, order[...]).reshape(NV, 8, 128).astype(bf16)
+    products = jnp.stack([dot_nt(tiles[q], kernels[q]) for q in range(NV)])
     products = jnp.where(wide_lane // 64 == wide_row // 2, products, 0.0)
     products = products[:, :, 0:128] + products[:, :, 128:256]
     products = products + pltpu.roll(products, 64, 2)
@@ -658,7 +681,7 @@
         copy.wait_send()
     out_image.wait()
     out_coeffs.wait()
-    for name in "abcdefghitu":
+    for name in "abcdefgitu":
         for part in range(2 if name in "bcdefg" else 1):
             finish(r, name, part, NB if name in "deu" else NV, 0)
     for part in range(2):
@@ -684,22 +707,22 @@
     here_down_hi=((384, 256), bf16),
     here_down_lo=((384, 256), bf16),
     sent_a=((1, NV, 8, 128), bf16), got_a=((1, NV, 8, 128), bf16),
-    sent_i=((1, NV, 1, 128), f32), got_i=((1, NV, 1, 128), f32),
+    sent_i=((1, 128), f32), got_i=((1, NV, 1, 128), f32),
     sent_b=(VIS_TILE, bf16), got_b=(VIS_TILE, bf16),
     sent_c=(VIS_TILE, bf16), got_c=(VIS_TILE, bf16),
     sent_d=(BAND_TILE, bf16), got_d=(BAND_TILE, bf16),
     sent_e=(BAND_TILE, bf16), got_e=(BAND_TILE, bf16),
     sent_f=(VIS_TILE, bf16), got_f=(VIS_TILE, bf16),
     sent_l=((2, 8, 8, 128), bf16), got_l=((2, NV, 8, 128), bf16),
-    sent_g=(VIS_TILE, bf16), got_g=(VIS_TILE, bf16),
-    sent_h=((1, NV, 8, 128), bf16), got_h=((1, NV, 8, 128), bf16),
+    sent_g=((2, NV, 16, 128), bf16), got_g=((2, NV, 16, 128), bf16),
+    hots=((4, 128, 1024), bf16), blocks=((4, 128, 1024), bf16), reorder=((256, 256), bf16),
     sent_t=((1, 128), f32), got_t=((1, NV, 1, 128), f32),
     sent_u=((1, 128), f32), got_u=((1, NB, 1, 128), f32),
     weights=((NV, 8, 256), bf16), twist_col=((8, 2, 16, 128), f32), coef_rows=((16, 2048), f32),
     got_coef=((16, 2048), f32), got_rows=((8, IMG), f32),
     raw_here=((16, IMG), f32), extrap=((2, 8, IMG), f32), coeffs_here=((4, 8, 2048), f32),
-    onehot=((256, 512), bf16), mid=((2, 32, 2, 8, 128), f32),
-    **{"sem_" + n: 4 for n in list("abcdefghiltu") + ["coef", "rows", "out"]},
+    mid=((2, 32, 2, 8, 128), f32),
+    **{"sem_" + n: 4 for n in list("abcdefgiltu") + ["coef", "rows", "out"]},
     sem_in=len(STAGED),
 )
 

time: 89.2 us -> 82.3 us (0.923)
  Pallas kernels: 88.5 us -> 81.6 us
    pallas_call x1, Pallas kernels: 86.6 us -> 79.7 us  [step(): pl.pallas_call(step_kernel, out_shape=(jax.ShapeDtypeStruct((16, IMG), f3...]
where the time goes in v6:
time: 82.3 us; the launch traced here: 82.2 us
  Pallas kernels  81.6 us (99%)
    pallas_call x1, Pallas kernels, step(): pl.pallas_call(step_kernel, out_shape=(jax.ShapeDtypeStruct((16, IMG), f3...  79.7 us
    pallas_call x1, Pallas kernels, closing(): pl.pallas_call(closing_kernel, out_shape=tuple((jax.ShapeDtypeStruct(x.sh...  1.83 us

profile of v6, /device:TPU:1, one launch (start us, length us, event | category | flops | bytes accessed | tf_op | source)
XLA Modules:
  0.0 82.2 jit_solution(8518069913975063114)
XLA Ops:
  0.6 79.7 %shard_map.220 = (f32[16,4096]{1,0:T(8,128)}, f32[4,8,2048]{2,1,0:T(8,128)}, f32[32,4,2,32]{3,2,1,0:T(2,128)}, f32[1,128]{1,0:T(1,128)}) custom-call(bf16[32,256,128]{2,1,0:T(8,128)(2,1)} %bitcast.8, f32[4,8,2048]{2,1,0:T(8,128)} %refs_1_.1, f32[16,4096]{1,0:T(8,128)} %refs_2_.1, bf16[512,256]{1,0:T(8,128)(2,1)} %constant.32.clone.refs_3_, ...), custom_call_target="tpu_custom_call" | custom-call | tf_op jit(solution)/shard_map/pallas_call | solution.py:739
  80.4 1.8 %shard_map.221 = (f32[16,4096]{1,0:T(8,128)}, f32[4,8,2048]{2,1,0:T(8,128)}, f32[32,4,2,32]{3,2,1,0:T(2,128)}) custom-call(f32[16,4096]{1,0:T(8,128)} %get-tuple-element.10.refs_0_, f32[4,8,2048]{2,1,0:T(8,128)} %get-tuple-element.11.refs_1_, f32[32,4,2,32]{3,2,1,0:T(2,128)} %get-tuple-element.12.refs_2_, f32[1,128]{1,0:T(1,128)} %get-tuple-element.13.refs_3_), custom_call_target="tpu_custom_call" | custom-call | tf_op jit(solution)/shard_map/pallas_call | solution.py:791

commit v7 on v6

--- a/solution.py
+++ b/solution.py
@@ -213,7 +213,7 @@
     return (x ^ x // 2) + n // 4 * 4
 
 
-def launch(r, name, part, axis, count, me, same=False):
+def launch(r, name, part, axis, count, me, same=False, shared=1):
     sent, landed, sems = r["sent_" + name], r["got_" + name].at[part], r["sem_" + name]
     if not same:
         sent = sent.at[part]
@@ -221,7 +221,7 @@
     def body(step, carry):
         peer = me ^ far_first(count - step, count)
         pltpu.make_async_remote_copy(
-            src_ref=sent if same else sent.at[peer],
+            src_ref=sent if same else sent.at[peer // shared],
             dst_ref=landed.at[me],
             send_sem=sems.at[2 * part],
             recv_sem=sems.at[2 * part + 1],
@@ -231,7 +231,7 @@
         return carry
 
     lax.fori_loop(1, count, body, 0)
-    landed[me] = sent[...] if same else sent[me]
+    landed[me] = sent[...] if same else sent[me // shared]
 
 
 def rest_copy(r, part, low, me):
@@ -339,6 +339,8 @@
     row, col = (lax.broadcasted_iota(jnp.int32, (256, 256), n) for n in range(2))
     source = row // 8 % 8 * 32 + row % 2 * 16 + row // 64 * 4 + row % 8 // 2
     r["reorder"][...] = (col == source).astype(f32).astype(bf16)
+    source = col // 8 % 8 * 32 + col % 2 * 16 + col // 64 * 4 + col % 8 // 2
+    backwards = (row == source).astype(f32).astype(bf16)
     r["blocks"][...] = jnp.zeros((4, 128, 1024), bf16)
     row_slot = lax.broadcasted_iota(jnp.int32, (256, 128), 0) % 8 // 2
     fact = lax.broadcasted_iota(jnp.int32, (256, 128), 1)
@@ -374,41 +376,28 @@
         one = jnp.sum(jnp.where(eye, one, 0.0), axis=1, keepdims=True)
         twist_col[:, c] = jnp.broadcast_to(one, (128, 128)).reshape(8, 16, 128)
 
+    order = r["order"]
     kernels = staged("kernels")
-    for q in range(NV):
-        r["sent_a"][0, q] = dot(r["weights"][q], kernels[q]).astype(bf16)
+    contrib = jnp.concatenate(
+        [dot(r["weights"][q], kernels[q]) for q in range(NV)], axis=0
+    ).astype(bf16)
+    contrib = dot(backwards, dot_nt(contrib, order[...]).astype(bf16))
+    groups = swap_groups([contrib[16 * n : 16 * n + 16] for n in range(16)], 8)
+    for part in range(2):
+        for low in range(8):
+            r["sent_b"][part, low] = groups[8 * part + low].astype(bf16)
     coef = staged("coef")
     for part in range(4):
         r["coef_rows"][3 * part : 3 * part + 3] = coef[part, 5:8, :]
     r["coef_rows"][12:16] = jnp.zeros((4, 2048), f32)
     r["got_l"][...] = jnp.zeros((2, NV, 8, 128), bf16)
+
     pl.semaphore_wait(barrier, NV + NB)
     launch(r, "i", 0, "vis", NV, vis_me, same=True)
-    launch(r, "a", 0, "vis", NV, vis_me)
+    for part in range(2):
+        launch(r, "b", part, "vis", NV, vis_me, shared=4)
     coef_copy = to_neighbour(r["coef_rows"], r["got_coef"], r["sem_coef"], following)
-
-    order = r["order"]
     positions = arrived(r, "i", 0, NV)[...].reshape(NV, 128)
-    where_to = per_row(positions, 32 * row_slot + vis_me)
-    where_to = jnp.broadcast_to(where_to, (256, 128))
-    lane = lax.broadcasted_iota(jnp.int32, (256, 128), 1).astype(f32)
-    is_imag = lax.broadcasted_iota(jnp.int32, (256, 128), 0) % 2 == 1
-    hots = [(where_to == lane + float(128 * g - 256)).astype(f32) for g in range(4)]
-    real_hots = [jnp.where(is_imag, 0.0, h).astype(bf16) for h in hots]
-    imag_hots = [jnp.where(is_imag, h, 0.0).astype(bf16) for h in hots]
-    hots = jnp.concatenate(real_hots + imag_hots, axis=1)
-    contrib = arrived(r, "a", 0, NV)[...].astype(f32).reshape(256, 128).astype(bf16)
-    turned = dot_nt(order[...], contrib).astype(bf16)
-    for part in range(2):
-        grid = dot(turned[64 * part : 64 * part + 64], hots)
-        for c in range(2):
-            for g in range(4):
-                cols = slice(512 * c + 128 * g, 512 * c + 128 * g + 128)
-                for low in range(8):
-                    r["sent_b"][part, low * 4 + g, c] = grid[
-                        8 * low : 8 * low + 8, cols
-                    ].astype(bf16)
-        launch(r, "b", part, "vis", NV, vis_me)
 
     to_row = (
         lax.broadcasted_iota(jnp.int32, (128, 32), 0) // 4
@@ -447,15 +436,38 @@
         raw[:, cols] = sky[:, cols] - smooth[16 * n : 16 * n + 16]
 
     table_hi, table_lo = staged("table_hi"), staged("table_lo")
+    upper = lax.broadcasted_iota(jnp.int32, (16, 8, 128), 1) < 4
 
     def spread_of(landed):
         return jnp.concatenate(
             [landed[:, 0].reshape(256, 128), landed[:, 1].reshape(256, 128)], axis=1
         )
 
-    first = spread_of(arrived(r, "b", 0, NV))
+    def gridded(landed):
+        reals, imags = [], []
+        for n in (0, 2):
+            both = landed[:, 4 * n : 4 * n + 8, :].astype(f32).reshape(16, 2, 8, 128)
+            even, odd = both[:, 0], both[:, 1]
+            for slots in (
+                jnp.where(upper, even, pltpu.roll(odd, 4, 1)),
+                jnp.where(upper, pltpu.roll(even, 4, 1), odd),
+            ):
+                total = lax.dot_general(
+                    slots.reshape(128, 128).astype(bf16),
+                    r["hots"][len(reals) // 8],
+                    (((0,), (0,)), ((), ())),
+                    preferred_element_type=f32,
+                )
+                for q in range(8):
+                    cols = slice(128 * q, 128 * q + 128)
+                    reals.append(total[16 * q : 16 * q + 8, cols])
+                    imags.append(total[16 * q + 8 : 16 * q + 16, cols])
+        reals, imags = jnp.concatenate(reals, axis=0), jnp.concatenate(imags, axis=0)
+        return jnp.concatenate([reals, imags], axis=1).astype(bf16)
+
+    first = gridded(arrived(r, "b", 0, NV))
     ahead = dot(table_hi[:, 0:256], first) + dot(table_lo[:, 0:256], first)
-    second = spread_of(arrived(r, "b", 1, NV))
+    second = gridded(arrived(r, "b", 1, NV))
     for part in range(2):
         both = []
         for side in range(2):
@@ -611,7 +623,6 @@
         picked = [
             dot_nt(r["hots"][n], r["blocks"][n]).reshape(16, 8, 128) for n in range(4)
         ]
-        upper = lax.broadcasted_iota(jnp.int32, (16, 8, 128), 1) < 4
         chunks = []
         for n in (0, 2):
             one, two = picked[n], picked[n + 1]
@@ -681,7 +692,7 @@
         copy.wait_send()
     out_image.wait()
     out_coeffs.wait()
-    for name in "abcdefgitu":
+    for name in "bcdefgitu":
         for part in range(2 if name in "bcdefg" else 1):
             finish(r, name, part, NB if name in "deu" else NV, 0)
     for part in range(2):
@@ -706,9 +717,8 @@
     here_table_lo=((1024, 512), bf16),
     here_down_hi=((384, 256), bf16),
     here_down_lo=((384, 256), bf16),
-    sent_a=((1, NV, 8, 128), bf16), got_a=((1, NV, 8, 128), bf16),
     sent_i=((1, 128), f32), got_i=((1, NV, 1, 128), f32),
-    sent_b=(VIS_TILE, bf16), got_b=(VIS_TILE, bf16),
+    sent_b=((2, 8, 16, 128), bf16), got_b=((2, NV, 16, 128), bf16),
     sent_c=(VIS_TILE, bf16), got_c=(VIS_TILE, bf16),
     sent_d=(BAND_TILE, bf16), got_d=(BAND_TILE, bf16),
     sent_e=(BAND_TILE, bf16), got_e=(BAND_TILE, bf16),
@@ -722,7 +732,7 @@
     got_coef=((16, 2048), f32), got_rows=((8, IMG), f32),
     raw_here=((16, IMG), f32), extrap=((2, 8, IMG), f32), coeffs_here=((4, 8, 2048), f32),
     mid=((2, 32, 2, 8, 128), f32),
-    **{"sem_" + n: 4 for n in list("abcdefgiltu") + ["coef", "rows", "out"]},
+    **{"sem_" + n: 4 for n in list("bcdefgiltu") + ["coef", "rows", "out"]},
     sem_in=len(STAGED),
 )
 

time: 82.3 us -> 79.1 us (0.961)
  Pallas kernels: 81.6 us -> 78.3 us
    pallas_call x1, Pallas kernels: 79.7 us -> 76.5 us  [step(): pl.pallas_call(step_kernel, out_shape=(jax.ShapeDtypeStruct((16, IMG), f3...]
where the time goes in v7:
time: 79.1 us; the launch traced here: 79 us
  Pallas kernels  78.3 us (99%)
    pallas_call x1, Pallas kernels, step(): pl.pallas_call(step_kernel, out_shape=(jax.ShapeDtypeStruct((16, IMG), f3...  76.5 us
    pallas_call x1, Pallas kernels, closing(): pl.pallas_call(closing_kernel, out_shape=tuple((jax.ShapeDtypeStruct(x.sh...  1.83 us

profile of v7, /device:TPU:1, one launch (start us, length us, event | category | flops | bytes accessed | tf_op | source)
XLA Modules:
  0.0 79.0 jit_solution(1389623751759137463)
XLA Ops:
  0.6 76.5 %shard_map.220 = (f32[16,4096]{1,0:T(8,128)}, f32[4,8,2048]{2,1,0:T(8,128)}, f32[32,4,2,32]{3,2,1,0:T(2,128)}, f32[1,128]{1,0:T(1,128)}) custom-call(bf16[32,256,128]{2,1,0:T(8,128)(2,1)} %bitcast.8, f32[4,8,2048]{2,1,0:T(8,128)} %refs_1_.1, f32[16,4096]{1,0:T(8,128)} %refs_2_.1, bf16[512,256]{1,0:T(8,128)(2,1)} %constant.32.clone.refs_3_, ...), custom_call_target="tpu_custom_call" | custom-call | tf_op jit(solution)/shard_map/pallas_call | solution.py:749
  77.1 1.8 %shard_map.221 = (f32[16,4096]{1,0:T(8,128)}, f32[4,8,2048]{2,1,0:T(8,128)}, f32[32,4,2,32]{3,2,1,0:T(2,128)}) custom-call(f32[16,4096]{1,0:T(8,128)} %get-tuple-element.10.refs_0_, f32[4,8,2048]{2,1,0:T(8,128)} %get-tuple-element.11.refs_1_, f32[32,4,2,32]{3,2,1,0:T(2,128)} %get-tuple-element.12.refs_2_, f32[1,128]{1,0:T(1,128)} %get-tuple-element.13.refs_3_), custom_call_target="tpu_custom_call" | custom-call | tf_op jit(solution)/shard_map/pallas_call | solution.py:801
